TPU v7x, 32 devices: a whole 2x2x4 slice. The times are simulated.
32 devices in a mesh: section: 8 (over z, core), row: 4 (over y, x).
Axes of the slice: x: 2, y: 2, z: 4, core: 2. Of those that a mesh axis runs over, the one named last changes fastest.
Arguments:
- section_inputs: bfloat16 [8, 512, 2048], P('section', 'row'), may hold values from -6 to 6
- fresh_group: bfloat16 [512, 2048], P('row'), may hold values from -6 to 6
- resident_state: float32 [8, 8, 128, 128], P('section'), may hold values from -81.4587 to 81.4587
- qkv_weight: bfloat16 [8, 2048, 3072], P('section', 'row'), may hold values from -0.125 to 0.125
- out_weight: bfloat16 [8, 1024, 2048], P('section', 'row'), may hold values from -0.1875 to 0.1875
- input_gain: float32 [8, 2048], P('section'), may hold values from 0.1 to 1.9
- head_gain: float32 [8, 1024], P('section'), may hold values from 0.1 to 1.9
Outputs:
- section_outputs: bfloat16 [8, 512, 2048], P('section', 'row')
- final_state: float32 [8, 8, 128, 128], P('section')
All inputs are finite; a program needn't handle non-finite values.
Results may differ from a plain program's by a relative error of at most 0.01.
Values may be sent and summed in bfloat16 or wider, within the bound.
No kernel may reach another device: no remote copies, remote signals or barrier semaphores. Data moves between devices by JAX's collectives and lax.ppermute only.
A program may use at most 64 MiB of HBM per device.

v0:
```python
import jax
import jax.numpy as jnp
from jax import lax
from jax.sharding import PartitionSpec as P


def passed_along(value, axis, by):
    peers = lax.axis_size(axis)
    pairs = [(i, i + by) for i in range(peers) if 0 <= i + by < peers]
    return lax.ppermute(value, axis, pairs)


def layer(inputs, state, qkv_full, out_full, input_gain, head_gain):
    rows = inputs.shape[0]
    heads = state.shape[0]
    head_size = state.shape[1]
    width = heads * head_size
    highest = lax.Precision.HIGHEST
    wide = inputs.astype(jnp.float32)
    normed = (
        wide * lax.rsqrt(jnp.mean(wide * wide, axis=-1, keepdims=True) + 1e-05) * input_gain
    ).astype(jnp.bfloat16)
    projected = jnp.dot(normed, qkv_full, preferred_element_type=jnp.float32)
    queries = jax.nn.silu(projected[:, :width]).astype(jnp.bfloat16).reshape(rows, heads, head_size)
    key_rows = (
        jax.nn.silu(projected[:, width : 2 * width])
        .astype(jnp.bfloat16)
        .reshape(rows, heads, head_size)
    )
    value_rows = projected[:, 2 * width :].astype(jnp.bfloat16).reshape(rows, heads, head_size)
    own_state = jnp.einsum("jhd,jhe->hde", key_rows, value_rows, preferred_element_type=jnp.float32)
    every = lax.all_gather(own_state[None].astype(jnp.bfloat16), "row", axis=0, tiled=True).astype(
        jnp.float32
    )
    order = lax.iota(jnp.int32, every.shape[0])
    earlier = (order < lax.axis_index("row")).astype(jnp.float32)
    before = jnp.sum(every * earlier[:, None, None, None], axis=0)
    total = jnp.sum(every, axis=0)
    prefix = state + before
    carried = jnp.einsum("ihd,hde->ihe", queries.astype(jnp.float32), prefix, precision=highest)
    scores = jnp.einsum("ihd,jhd->hij", queries, key_rows, preferred_element_type=jnp.float32)
    causal = lax.broadcasted_iota(jnp.int32, (rows, rows), 0) >= lax.broadcasted_iota(
        jnp.int32, (rows, rows), 1
    )
    weights = jnp.where(causal[None], scores, 0.0).astype(jnp.bfloat16)
    local = jnp.einsum("hij,jhe->ihe", weights, value_rows, preferred_element_type=jnp.float32)
    attended = carried + local
    scaled = attended * lax.rsqrt(jnp.mean(attended * attended, axis=-1, keepdims=True) + 1e-06)
    head_out = (scaled.reshape(rows, width) * head_gain).astype(jnp.bfloat16)
    result = (wide + jnp.dot(head_out, out_full, preferred_element_type=jnp.float32)).astype(
        jnp.bfloat16
    )
    return (result, state + total)


def body(
    section_inputs, fresh_group, resident_state, qkv_weight, out_weight, input_gain, head_gain
):
    qkv_full, out_full = (
        lax.all_gather(qkv_weight[0], "row", axis=0, tiled=True),
        lax.all_gather(out_weight[0], "row", axis=0, tiled=True),
    )
    first_out, first_state = layer(
        section_inputs[0], resident_state[0], qkv_full, out_full, input_gain[0], head_gain[0]
    )
    arrived = passed_along(first_out, "section", 1)
    second_in = jnp.where(lax.axis_index("section") == 0, fresh_group, arrived)
    second_out, second_state = layer(
        second_in, first_state, qkv_full, out_full, input_gain[0], head_gain[0]
    )
    return (second_out[None], second_state[None])


def solution(mesh):
    in_specs = (
        P("section", "row", None),
        P("row", None),
        P("section", None, None, None),
        P("section", "row", None),
        P("section", "row", None),
        P("section", None),
        P("section", None),
    )
    out_specs = (P("section", "row", None), P("section", None, None, None))
    return jax.shard_map(body, mesh=mesh, in_specs=in_specs, out_specs=out_specs, check_vma=False)
```

profile of v0, /device:TPU:0, one launch (start us, length us, event | category | flops | bytes accessed | tf_op | source)
XLA Modules:
  0.0 287.3 jit_solution(16072753598451398039)
XLA Ops:
  7.2 0.7 all-gather.9.cloned.1.call-update
  7.9 1.2 fusion.32
  9.2 125.8 %all-gather.9.cloned.1.call-done = bf16[1,2048,3072]{2,1,0:T(8,128)(2,1)} async-done(((bf16[1,512,3072]{2,1,0:T(8,128)(2,1)}), bf16[1,2048,3072]{2,1,0:T(8,128)(2,1)}) %all-gather.9.cloned.1.call-update) | async-done | bytes 12582928 | tf_op jit(solution)/shard_map/all_gather | solution.py:60
  135.0 6.7 %fusion.2 = f32[128,3072]{1,0:T(8,128)S(1)} fusion(bf16[1,2048,3072]{2,1,0:T(8,128)(2,1)} %all-gather.9.cloned.1.call-done, bf16[1,128,2048]{2,1,0:T(8,128)(2,1)} %param.7, f32[2048]{0:T(1024)} %bitcast.105, f32[128]{0:T(128)S(1)} %add_rsqrt_fusion.3), kind=kOutput, calls=%fused_computation.2 | convolution fusion | flops 1611661312 | bytes 14688768 | tf_op jit(solution)/shard_map/dot_general | solution.py:23
  141.7 0.3 fusion.56
  142.0 0.2 copy.31
  142.2 0.2 copy.33
  142.3 1.0 convolution_convert_fusion.1
  143.4 0.0 all-gather.13.cloned.1.call-start
  143.4 0.7 all-gather.13.cloned.1.call-update
  144.2 25.8 %all-gather.11.cloned.1.call-done = bf16[32,128,128]{2,1,0:T(8,128)(2,1)} async-done(((bf16[8,128,128]{2,1,0:T(8,128)(2,1)}), bf16[32,128,128]{2,1,0:T(8,128)(2,1)}) %all-gather.11.cloned.1.call-update) | async-done | bytes 1048592 | tf_op jit(solution)/shard_map/all_gather | solution.py:32
  170.0 1.7 convert_reduce_fusion.1
  171.8 0.6 fusion.40
  172.4 0.5 multiply_reduce_fusion.1
  172.9 0.2 fusion.38
  173.1 51.3 %all-gather.13.cloned.1.call-done = bf16[1,1024,2048]{2,1,0:T(8,128)(2,1)} async-done(((bf16[1,256,2048]{2,1,0:T(8,128)(2,1)}), bf16[1,1024,2048]{2,1,0:T(8,128)(2,1)}) %all-gather.13.cloned.1.call-update) | async-done | bytes 4194320 | tf_op jit(solution)/shard_map/all_gather | solution.py:61
  224.5 2.9 %fusion.17 = bf16[128,2048]{1,0:T(8,128)(2,1)S(1)} fusion(bf16[128,1024]{0,1:T(8,128)(2,1)S(1)} %fusion.38, bf16[1,1024,2048]{2,1,0:T(8,128)(2,1)} %all-gather.13.cloned.1.call-done, bf16[1,128,2048]{2,1,0:T(8,128)(2,1)S(1)} %copy-done), kind=kOutput, calls=%fused_computation.15 | convolution fusion | flops 537657344 | bytes 5505024 | tf_op jit(solution)/shard_map/dot_general | solution.py:50
  227.4 1.6 collective-permute-start
  229.0 1.5 collective-permute-done
  230.5 0.3 fusion.29
  230.8 6.5 %fusion = f32[128,3072]{1,0:T(8,128)S(1)} fusion(bf16[1,2048,3072]{2,1,0:T(8,128)(2,1)} %all-gather.9.cloned.1.call-done, bf16[128,2048]{1,0:T(8,128)(2,1)S(1)} %get-tuple-element.7, f32[128]{0:T(128)S(1)} %add_rsqrt_fusion.2, f32[2048]{0:T(1024)S(1)} %bitcast.106), kind=kOutput, calls=%fused_computation | convolution fusion | flops 1611661312 | bytes 14688768 | tf_op jit(solution)/shard_map/dot_general | solution.py:23
  237.3 0.3 fusion.57
  237.6 0.2 copy.32
  237.8 0.2 copy.34
  238.0 1.0 convolution_convert_fusion
  239.0 34.0 %all-gather.15.cloned.1.call-done = bf16[32,128,128]{2,1,0:T(8,128)(2,1)} async-done(((bf16[8,128,128]{2,1,0:T(8,128)(2,1)}), bf16[32,128,128]{2,1,0:T(8,128)(2,1)}) %all-gather.15.cloned.1.call-update) | async-done | bytes 1048592 | tf_op jit(solution)/shard_map/all_gather | solution.py:32
  273.1 1.7 convert_reduce_fusion
  274.8 0.9 bitcast_add_fusion
  275.7 0.6 fusion.42
  276.3 0.5 multiply_reduce_fusion
  276.8 0.2 fusion.37
  277.0 3.7 %fusion.20 = bf16[1,128,2048]{2,1,0:T(8,128)(2,1)} fusion(bf16[128,1024]{0,1:T(8,128)(2,1)S(1)} %fusion.37, bf16[1,1024,2048]{2,1,0:T(8,128)(2,1)} %all-gather.13.cloned.1.call-done, bf16[128,2048]{1,0:T(8,128)(2,1)S(1)} %get-tuple-element.7), kind=kOutput, calls=%fused_computation.16 | convolution fusion | flops 537657344 | bytes 5505024 | tf_op jit(solution)/shard_map/dot_general | solution.py:50
  (25 shorter events, 0.4 us)
Async XLA Ops:
  7.2 127.8 %all-gather.9.cloned.1.call-start = ((), (), s32[]{:S(2)}) async-start(), calls=%async_computation | async-start | bytes 15728640 | tf_op jit(solution)/shard_map/all_gather | solution.py:60
  7.9 162.1 %all-gather.11.cloned.1.call-start = ((), (), s32[]{:S(2)}) async-start(), calls=%async_computation.1 | async-start | bytes 1310720 | tf_op jit(solution)/shard_map/all_gather | solution.py:32
  141.6 30.1 %copy-start.1 = (f32[1,8,128,128]{3,2,1,0:T(8,128)S(1)}, f32[1,8,128,128]{3,2,1,0:T(8,128)}, u32[]{:S(2)}) copy-start(f32[1,8,128,128]{3,2,1,0:T(8,128)} %param.9) | copy-start | bytes 1572868
  143.3 29.6 %copy-start.4 = (f32[1,1024]{1,0:T(1,128)S(1)}, f32[1,1024]{1,0:T(1,128)}, u32[]{:S(2)}) copy-start(f32[1,1024]{1,0:T(1,128)} %param.13) | copy-start | bytes 12292
  143.4 81.1 %copy-start = (bf16[1,128,2048]{2,1,0:T(8,128)(2,1)S(1)}, bf16[1,128,2048]{2,1,0:T(8,128)(2,1)}, u32[]{:S(2)}) copy-start(bf16[1,128,2048]{2,1,0:T(8,128)(2,1)} %param.7) | copy-start | bytes 1572868
  143.4 81.1 %all-gather.13.cloned.1.call-start = ((), (), s32[]{:S(2)}) async-start(), calls=%async_computation.2 | async-start | bytes 5242880 | tf_op jit(solution)/shard_map/all_gather | solution.py:61
  144.1 129.0 %all-gather.15.cloned.1.call-start = ((), (), s32[]{:S(2)}) async-start(), calls=%async_computation.3 | async-start | bytes 1310720 | tf_op jit(solution)/shard_map/all_gather | solution.py:32
  172.8 57.7 %copy-start.2 = (bf16[128,2048]{1,0:T(8,128)(2,1)S(1)}, bf16[128,2048]{1,0:T(8,128)(2,1)}, u32[]{:S(2)}) copy-start(bf16[128,2048]{1,0:T(8,128)(2,1)} %param.8) | copy-start | bytes 1572868
  172.9 57.9 %copy-start.3 = (f32[1,2048]{1,0:T(1,128)S(1)}, f32[1,2048]{1,0:T(1,128)}, u32[]{:S(2)}) copy-start(f32[1,2048]{1,0:T(1,128)} %param.12) | copy-start | bytes 24580
  227.4 3.1 %collective-permute-start = (bf16[128,2048]{1,0:T(8,128)(2,1)S(1)}, bf16[128,2048]{1,0:T(8,128)(2,1)S(1)}, u32[]{:S(2)}, u32[]{:S(2)}) collective-permute-start(bf16[128,2048]{1,0:T(8,128)(2,1)S(1)} %fusion.17), channel_id=1, source_target_pairs={{0,4},{4,8},{8,12},{12,16},{16,20},{20,24},{24,28},{1,5},{5,9},{9,... | collective-permute-start | bytes 1572872 | tf_op jit(solution)/shard_map/ppermute | solution.py:10
Sparse Core Ops, SparseCore 0:
  9.8 125.0 all-gather.8
  143.5 26.4 all-gather.10
  171.9 52.5 all-gather.12
  239.2 33.8 all-gather.14
where the time goes:
time: 288 us; the launch traced here: 287 us
  waiting for transfers between devices  240 us (83%)
  matrix products  24 us (8%)
  between operations  14 us (5%)
  other arithmetic  6.95 us (2%)
    all_gather x1, waiting for transfers between devices, body(): lax.all_gather(qkv_weight[0], 'row', axis=0, tiled=True)  126 us
    all_gather x2, waiting for transfers between devices, layer(): lax.all_gather(own_state[None].astype(jnp.bfloat16), 'row', axis=0, tiled...  59.8 us
    all_gather x1, waiting for transfers between devices, body(): lax.all_gather(out_weight[0], 'row', axis=0, tiled=True)  51.3 us
    dot_general x2, matrix products, layer(): projected = jnp.dot(normed, qkv_full, preferred_element_type=jnp.float32)  13.2 us
    dot_general x2, matrix products, layer(): jnp.dot(head_out, out_full, preferred_element_type=jnp.float32)  6.66 us
  transfers between devices with their start and end apart: 5, of which 5 were waited for; matrix products, arithmetic and copies ran while one was open for 1% of the time, Pallas kernels for 0%

commit v1 on v0

v1 whole, which is shorter than its diff:
```python
import functools

import jax
import jax.numpy as jnp
from jax import lax
from jax.experimental import pallas as pl
from jax.experimental.pallas import tpu as pltpu
from jax.sharding import PartitionSpec as P


VMEM = pl.BlockSpec(memory_space=pltpu.VMEM)
SMEM = pl.BlockSpec(memory_space=pltpu.SMEM)
F32 = jnp.float32
BF16 = jnp.bfloat16


def passed_along(value, axis, by):
    peers = lax.axis_size(axis)
    pairs = [(i, i + by) for i in range(peers) if 0 <= i + by < peers]
    return lax.ppermute(value, axis, pairs)


def layer(inputs, state, qkv_full, out_full, input_gain, head_gain):
    rows = inputs.shape[0]
    heads = state.shape[0]
    head_size = state.shape[1]
    width = heads * head_size
    highest = lax.Precision.HIGHEST
    wide = inputs.astype(F32)
    normed = (
        wide * lax.rsqrt(jnp.mean(wide * wide, axis=-1, keepdims=True) + 1e-05) * input_gain
    ).astype(BF16)
    projected = jnp.dot(normed, qkv_full, preferred_element_type=F32)
    queries = jax.nn.silu(projected[:, :width]).astype(BF16).reshape(rows, heads, head_size)
    key_rows = (
        jax.nn.silu(projected[:, width : 2 * width]).astype(BF16).reshape(rows, heads, head_size)
    )
    value_rows = projected[:, 2 * width :].astype(BF16).reshape(rows, heads, head_size)
    own_state = jnp.einsum("jhd,jhe->hde", key_rows, value_rows, preferred_element_type=F32)
    every = lax.all_gather(own_state[None].astype(BF16), "row", axis=0, tiled=True).astype(F32)
    order = lax.iota(jnp.int32, every.shape[0])
    earlier = (order < lax.axis_index("row")).astype(F32)
    before = jnp.sum(every * earlier[:, None, None, None], axis=0)
    total = jnp.sum(every, axis=0)
    prefix = state + before
    carried = jnp.einsum("ihd,hde->ihe", queries.astype(F32), prefix, precision=highest)
    scores = jnp.einsum("ihd,jhd->hij", queries, key_rows, preferred_element_type=F32)
    causal = lax.broadcasted_iota(jnp.int32, (rows, rows), 0) >= lax.broadcasted_iota(
        jnp.int32, (rows, rows), 1
    )
    weights = jnp.where(causal[None], scores, 0.0).astype(BF16)
    local = jnp.einsum("hij,jhe->ihe", weights, value_rows, preferred_element_type=F32)
    attended = carried + local
    scaled = attended * lax.rsqrt(jnp.mean(attended * attended, axis=-1, keepdims=True) + 1e-06)
    head_out = (scaled.reshape(rows, width) * head_gain).astype(BF16)
    result = (wide + jnp.dot(head_out, out_full, preferred_element_type=F32)).astype(BF16)
    return (result, state + total)


def gathered_body(
    section_inputs, fresh_group, resident_state, qkv_weight, out_weight, input_gain, head_gain
):
    qkv_full, out_full = (
        lax.all_gather(qkv_weight[0], "row", axis=0, tiled=True),
        lax.all_gather(out_weight[0], "row", axis=0, tiled=True),
    )
    first_out, first_state = layer(
        section_inputs[0], resident_state[0], qkv_full, out_full, input_gain[0], head_gain[0]
    )
    arrived = passed_along(first_out, "section", 1)
    second_in = jnp.where(lax.axis_index("section") == 0, fresh_group, arrived)
    second_out, second_state = layer(
        second_in, first_state, qkv_full, out_full, input_gain[0], head_gain[0]
    )
    return (second_out[None], second_state[None])


def steps(section):
    return (1, 2) if section % 2 == 0 else (2, 1)


def along(value, axis, only=None):
    sections, rows = lax.axis_size("section"), lax.axis_size("row")
    pairs = [
        (s * rows + r, s * rows + (r ^ steps(s)[axis]))
        for s in range(sections)
        for r in range(rows)
        if only is None or s == only
    ]
    return lax.ppermute(value, ("section", "row"), pairs)


def to_next(value, over_a, over_b):
    sections, rows = lax.axis_size("section"), lax.axis_size("row")
    pairs = []
    for s in range(sections):
        to = (s + 1) % sections
        a, b = steps(to)
        pairs += [(s * rows + r, to * rows + (r ^ (a * over_a) ^ (b * over_b))) for r in range(rows)]
    return lax.ppermute(value, ("section", "row"), pairs)


def limit(mebibytes):
    return pltpu.CompilerParams(vmem_limit_bytes=mebibytes << 20)


def whereabouts(info_ref, count):
    info = info_ref[0]
    odd = info // (3 * count)
    return info % count, info // count % 3, 1 + odd, 2 - odd


def halve_kernel(count, info_ref, *refs):
    me, _, bit_a, bit_b = whereabouts(info_ref, count)
    sources, outs = refs[: len(refs) // 3], refs[len(refs) // 3 :]
    for i, source in enumerate(sources):
        depth = source.shape[1] // count
        for out_ref, low in zip(outs[2 * i :], (me & bit_b, (me & bit_b) ^ bit_b)):
            for part, block in enumerate((low, low | bit_a)):
                at = pl.multiple_of(block * depth, depth)
                out_ref[:, part * depth : (part + 1) * depth] = source[:, pl.ds(at, depth)]


def halve(info, count, *arrays):
    outs = [
        jax.ShapeDtypeStruct((x.shape[0], x.shape[1] // 2), x.dtype)
        for x in arrays
        for _ in range(2)
    ]
    return pl.pallas_call(
        functools.partial(halve_kernel, count),
        out_shape=outs,
        in_specs=[SMEM] + [VMEM] * len(arrays),
        out_specs=[VMEM] * len(outs),
        compiler_params=limit(6),
        name="halve",
    )(info, *arrays)


def cut_kernel(count, info_ref, w_ref, *out_refs):
    me, _, bit_a, bit_b = whereabouts(info_ref, count)
    cols = out_refs[0].shape[1] // 3
    for out_ref, offset in zip(out_refs, (0, bit_a, bit_b, bit_a | bit_b)):
        for c in range(3):
            at = pl.multiple_of((c * count + (me ^ offset)) * cols, cols)
            out_ref[:, c * cols : (c + 1) * cols] = w_ref[:, pl.ds(at, cols)]


def cut(info, weight, count):
    depth, cols3 = weight.shape
    return pl.pallas_call(
        functools.partial(cut_kernel, count),
        out_shape=[jax.ShapeDtypeStruct((depth, cols3 // count), BF16)] * 4,
        in_specs=[SMEM, VMEM],
        out_specs=[VMEM] * 4,
        compiler_params=limit(9),
        name="cut",
    )(info, weight)


def assemble(me, bit_a, bit_b, x_refs, x_all):
    offsets = (0, bit_a, bit_b, bit_a | bit_b)
    rows, width = x_refs[0].shape
    if width == x_all.shape[1]:
        for x_ref, offset in zip(x_refs, offsets):
            x_all[pl.ds(pl.multiple_of((me ^ offset) * rows, rows), rows), :] = x_ref[...]
        return
    block = rows // 2
    for j, x_ref in enumerate(x_refs):
        part = (me & bit_a) // bit_a
        columns = pl.ds(pl.multiple_of((part if j % 2 == 0 else 1 - part) * width, width), width)
        low = me & bit_b if j < 2 else (me & bit_b) ^ bit_b
        for t in range(2):
            at = pl.multiple_of((low | (t * bit_a)) * block, block)
            x_all[pl.ds(at, block), columns] = x_ref[t * block : (t + 1) * block, :]


def pair_weights(me, bit_a, w_refs, w_all):
    depth = w_refs[0].shape[0]
    second = (me & bit_a) // bit_a
    w_all[pl.ds(pl.multiple_of(second * depth, depth), depth), :] = w_refs[0][...]
    w_all[pl.ds(pl.multiple_of((1 - second) * depth, depth), depth), :] = w_refs[1][...]


def given_kernel(count, first, info_ref, gain_ref, *refs):
    me, _, bit_a, bit_b = whereabouts(info_ref, count)
    x_refs, refs = refs[:4], refs[4:]
    w_refs, refs = refs[: 1 + first], refs[1 + first :]
    out_ref, scaled_ref, x_all, refs = *refs[:3], refs[3:]
    w_all = refs[0] if first else w_refs[0]
    assemble(me, bit_a, bit_b, x_refs, x_all)
    if first:
        pair_weights(me, bit_a, w_refs, w_all)
    depth = scaled_ref.shape[1] // 2
    rows, tail = x_all.shape[0], out_ref.shape[0] - x_all.shape[0]
    total = None
    for part in range(2):
        at = pl.multiple_of(((me & bit_b) | (part * bit_a)) * depth, depth)
        columns = slice(part * depth, (part + 1) * depth)
        wide = x_all[:, columns].astype(F32)
        scaled_ref[:, columns] = (wide * gain_ref[:, pl.ds(at, depth)]).astype(BF16)
        term = lax.dot_general(
            jnp.ones((tail, depth), BF16),
            (wide * wide).astype(BF16),
            (((1,), (1,)), ((), ())),
            preferred_element_type=F32,
        )
        total = term if total is None else total + term
    out_ref[:rows, :] = jnp.dot(
        scaled_ref[...], w_all[...], preferred_element_type=F32
    ).astype(BF16)
    high = total.astype(BF16).astype(F32)
    line = lax.broadcasted_iota(jnp.int32, total.shape, 0)
    pair = jnp.where(line == 0, high, jnp.where(line == 1, total - high, 0.0))
    out_ref[rows:, :] = jnp.zeros((tail, out_ref.shape[1]), BF16)
    out_ref[rows:, :rows] = pair.astype(BF16)


def given_product(info, count, gain, x, w):
    first = len(w) > 1
    rows, half = x[0].size * len(x) * 2 // gain.shape[1], gain.shape[1] // 2
    cols = w[0].shape[1]
    outs = [jax.ShapeDtypeStruct((rows + 16, cols), BF16)]
    outs += [jax.ShapeDtypeStruct((rows, half), BF16)] * 2
    outs += [jax.ShapeDtypeStruct((half, cols), BF16)] if first else []
    return pl.pallas_call(
        functools.partial(given_kernel, count, first),
        out_shape=outs,
        in_specs=[SMEM] + [VMEM] * (1 + len(x) + len(w)),
        out_specs=[VMEM] * len(outs),
        cost_estimate=pl.CostEstimate(
            flops=2 * rows * half * cols, bytes_accessed=4 << 20, transcendentals=0
        ),
        compiler_params=limit(12),
        name="given_first" if first else "given_second",
    )(info, gain, *x, *w)


def own_kernel(count, first, info_ref, scaled_ref, *refs):
    me, _, bit_a, _ = whereabouts(info_ref, count)
    w_refs, refs = refs[: 1 + first], refs[1 + first :]
    out_ref = refs[0]
    w_all = refs[1] if first else w_refs[0]
    if first:
        pair_weights(me, bit_a, w_refs, w_all)
    out_ref[...] = jnp.dot(scaled_ref[...], w_all[...], preferred_element_type=F32)


def own_product(info, count, scaled, w):
    first = len(w) > 1
    rows, half = scaled.shape
    cols = w[0].shape[1]
    outs = [jax.ShapeDtypeStruct((rows, cols), F32)]
    outs += [jax.ShapeDtypeStruct((half, cols), BF16)] if first else []
    return pl.pallas_call(
        functools.partial(own_kernel, count, first),
        out_shape=outs,
        in_specs=[SMEM] + [VMEM] * (1 + len(w)),
        out_specs=[VMEM] * len(outs),
        cost_estimate=pl.CostEstimate(
            flops=2 * rows * half * cols, bytes_accessed=4 << 20, transcendentals=0
        ),
        compiler_params=limit(12),
        name="own_first" if first else "own_second",
    )(info, scaled, *w)


def attend_kernel(count, first, width, info_ref, *refs):
    own_ref, given_ref, got_ref, state_ref, gain_ref, refs = *refs[:5], refs[5:]
    if not first:
        resident_ref, refs = refs[0], refs[1:]
    ho_ref, new_state_ref, qkv = refs
    me, _, _, _ = whereabouts(info_ref, count)
    own, size = new_state_ref.shape[0], new_state_ref.shape[1]
    cols = own * size
    block = own_ref.shape[0] // count
    rows, square = own_ref.shape[0], None
    for ref in (given_ref, got_ref):
        tail = ref[rows:, :rows]
        term = lax.dot_general(
            tail,
            jnp.ones((tail.shape[0], 128), BF16),
            (((0,), (0,)), ((), ())),
            preferred_element_type=F32,
        )
        square = term if square is None else square + term
    scale = lax.rsqrt(square[:, :1] / width + 1e-05)
    for c in range(3):
        columns = slice(c * cols, (c + 1) * cols)
        part = (own_ref[:, columns] + got_ref[:rows, columns].astype(F32)) * scale
        if c < 2:
            part = part / (1.0 + jnp.exp(-part))
        qkv[:, columns] = part.astype(BF16)
    causal = lax.broadcasted_iota(jnp.int32, (block, block), 0) >= lax.broadcasted_iota(
        jnp.int32, (block, block), 1
    )
    gains = gain_ref[:, pl.ds(pl.multiple_of(me * cols, cols), cols)]
    for h in range(own):
        prefix = state_ref[me * own + h] if first else state_ref[h]
        for b in range(count):
            rows = slice(b * block, (b + 1) * block)
            q, k, v = (
                qkv[rows, c * cols + h * size : c * cols + (h + 1) * size] for c in range(3)
            )
            high = prefix.astype(BF16)
            low = (prefix - high.astype(F32)).astype(BF16)
            scores = lax.dot_general(
                q, k, (((1,), (1,)), ((), ())), preferred_element_type=F32
            )
            weights = jnp.where(causal, scores, 0.0).astype(BF16)
            attended = (
                jnp.dot(q, high, preferred_element_type=F32)
                + jnp.dot(q, low, preferred_element_type=F32)
                + jnp.dot(weights, v, preferred_element_type=F32)
            )
            mean = jnp.mean(attended * attended, axis=-1, keepdims=True)
            scaled = attended * lax.rsqrt(mean + 1e-06) * gains[:, h * size : (h + 1) * size]
            ho_ref[rows, h * size : (h + 1) * size] = scaled.astype(BF16)
            prefix = prefix + lax.dot_general(
                k, v, (((0,), (0,)), ((), ())), preferred_element_type=F32
            )
        new_state_ref[h] = prefix
        if not first:
            change = (prefix - resident_ref[me * own + h]).astype(BF16)
            ho_ref[count * block :, h * size : (h + 1) * size] = change


def attend(info, count, width, own, given, got, state, head_gain, resident=None):
    first = resident is None
    rows, cols3 = own.shape
    size = state.shape[-1]
    heads = cols3 // 3 // size
    ins = [info, own, given, got, state, head_gain] + ([] if first else [resident])
    outs = [
        jax.ShapeDtypeStruct((rows + (0 if first else size), heads * size), BF16),
        jax.ShapeDtypeStruct((heads, size, size), F32),
    ]
    return pl.pallas_call(
        functools.partial(attend_kernel, count, first, width),
        out_shape=outs,
        in_specs=[SMEM] + [VMEM] * (len(ins) - 1),
        out_specs=[VMEM] * len(outs),
        scratch_shapes=[pltpu.VMEM((rows, cols3), BF16)],
        cost_estimate=pl.CostEstimate(
            flops=10 * rows * heads * size * size, bytes_accessed=8 << 20, transcendentals=0
        ),
        compiler_params=limit(15),
        name="attend_first" if first else "attend_second",
    )(*ins)


def outgoing_kernel(count, mine, info_ref, *refs):
    ho_refs, w_refs, out_ref, lhs = refs[:2], refs[2:4], refs[4], refs[5]
    me, _, bit_a, bit_b = whereabouts(info_ref, count)
    low = me & bit_a if mine else (me & bit_a) ^ bit_a
    block, depth = ho_refs[0].shape[0] // count, ho_refs[0].shape[1]
    for t in range(2):
        at = pl.multiple_of((low | (t * bit_b)) * block, block)
        for i, ho_ref in enumerate(ho_refs):
            lhs[t * block : (t + 1) * block, i * depth : (i + 1) * depth] = ho_ref[
                pl.ds(at, block), :
            ]
    total = None
    for i, w_ref in enumerate(w_refs):
        term = jnp.dot(
            lhs[:, i * depth : (i + 1) * depth], w_ref[...], preferred_element_type=F32
        )
        total = term if total is None else total + term
    out_ref[...] = total.astype(out_ref.dtype)


def outgoing(info, count, heads, weights, mine):
    rows, depth = heads[0].shape[0] // 2, heads[0].shape[1]
    cols = weights[0].shape[1]
    return pl.pallas_call(
        functools.partial(outgoing_kernel, count, mine),
        out_shape=jax.ShapeDtypeStruct((rows, cols), F32 if mine else BF16),
        in_specs=[SMEM] + [VMEM] * 4,
        out_specs=VMEM,
        scratch_shapes=[pltpu.VMEM((rows, 2 * depth), BF16)],
        cost_estimate=pl.CostEstimate(
            flops=4 * rows * depth * cols, bytes_accessed=4 << 20, transcendentals=0
        ),
        compiler_params=limit(9),
        name="outgoing_mine" if mine else "outgoing_given",
    )(info, *heads, *weights)


def quarter_kernel(count, info_ref, own_ref, got_ref, x_ref, fresh_ref, partner_ref, *refs):
    next_mine, next_other, quarter = refs
    me, place, bit_a, bit_b = whereabouts(info_ref, count)
    block, depth = fresh_ref.shape[0], own_ref.shape[1] // 2
    second = (me & bit_b) // bit_b
    here = pl.ds(pl.multiple_of(second * block, block), block)
    there = pl.ds(pl.multiple_of((1 - second) * block, block), block)
    for t in range(2):
        rows = slice(t * block, (t + 1) * block)
        at = pl.multiple_of(((me & bit_a) | (t * bit_b)) * block, block)
        x = x_ref[pl.ds(at, block), :].astype(F32)
        quarter[rows, :] = (x + own_ref[rows, :] + got_ref[rows, :].astype(F32)).astype(BF16)

    @pl.when(place == 1)
    def _():
        quarter[here, :] = fresh_ref[...]
        quarter[there, :] = partner_ref[...]

    part = (me & bit_a) // bit_a
    next_mine[...] = quarter[:, pl.ds(pl.multiple_of(part * depth, depth), depth)]
    next_other[...] = quarter[:, pl.ds(pl.multiple_of((1 - part) * depth, depth), depth)]


def quarter(info, count, own, got, x, fresh, fresh_partner):
    rows, cols = own.shape
    block = jax.ShapeDtypeStruct((rows, cols // 2), BF16)
    return pl.pallas_call(
        functools.partial(quarter_kernel, count),
        out_shape=(block, block),
        in_specs=[SMEM] + [VMEM] * 5,
        out_specs=(VMEM, VMEM),
        scratch_shapes=[pltpu.VMEM((rows, cols), BF16)],
        cost_estimate=pl.CostEstimate(
            flops=4 * rows * cols, bytes_accessed=4 << 20, transcendentals=0
        ),
        compiler_params=limit(9),
        name="quarter",
    )(info, own, got, x, fresh, fresh_partner)


def deal_kernel(count, info_ref, *refs):
    ho_refs, w_refs, x_ref, refs = refs[:2], refs[2:4], refs[4], refs[5:]
    keep_ref, a_ref, b_ref, cross_ref, product = refs
    me, _, bit_a, bit_b = whereabouts(info_ref, count)
    rows, block = x_ref.shape[0], keep_ref.shape[0]
    total = None
    for ho_ref, w_ref in zip(ho_refs, w_refs):
        term = jnp.dot(ho_ref[:rows, :], w_ref[...], preferred_element_type=F32)
        total = term if total is None else total + term
    product[...] = total
    for out_ref, offset, residual in (
        (cross_ref, bit_a | bit_b, False),
        (a_ref, bit_a, False),
        (b_ref, bit_b, True),
        (keep_ref, 0, True),
    ):
        at = pl.ds(pl.multiple_of((me ^ offset) * block, block), block)
        out = product[at, :]
        if residual:
            out = out + x_ref[at, :].astype(F32)
        out_ref[:block, :] = out.astype(out_ref.dtype)
    size, cols = ho_refs[0].shape[0] - rows, ho_refs[0].shape[1]
    fold = x_ref.shape[1] // cols
    high = size // fold
    for i, ho_ref in enumerate(ho_refs):
        for q in range(fold):
            a_ref[block + i * high : block + (i + 1) * high, q * cols : (q + 1) * cols] = ho_ref[
                rows + q * high : rows + (q + 1) * high, :
            ]


def deal(info, count, heads, weights, x):
    rows, cols = x.shape
    block = rows // count
    size = heads[0].shape[0] - rows
    part = jax.ShapeDtypeStruct((block, cols), BF16)
    wide = jax.ShapeDtypeStruct((block, cols), F32)
    more = jax.ShapeDtypeStruct((block + 2 * size * heads[0].shape[1] // cols, cols), BF16)
    return pl.pallas_call(
        functools.partial(deal_kernel, count),
        out_shape=(wide, more, wide, part),
        in_specs=[SMEM] + [VMEM] * 5,
        out_specs=(VMEM,) * 4,
        scratch_shapes=[pltpu.VMEM((rows, cols), F32)],
        cost_estimate=pl.CostEstimate(
            flops=4 * rows * heads[0].shape[1] * cols, bytes_accessed=4 << 20, transcendentals=0
        ),
        compiler_params=limit(12),
        name="deal",
    )(info, *heads, *weights, x)


def combine_kernel(mine_ref, got_ref, out_ref):
    out_ref[...] = (mine_ref[...] + got_ref[...].astype(F32)).astype(BF16)


def combine(mine, got):
    return pl.pallas_call(
        combine_kernel,
        out_shape=jax.ShapeDtypeStruct(got.shape, BF16),
        in_specs=[VMEM, VMEM],
        out_specs=VMEM,
        compiler_params=limit(4),
        name="combine",
    )(mine, got)


def last_kernel(count, info_ref, keep_ref, a_ref, b_ref, heads_ref, *refs):
    resident_ref, own_ref, out_ref, final_ref = refs
    me, _, bit_a, bit_b = whereabouts(info_ref, count)
    block, width = out_ref.shape
    depth = width // count
    for t in range(2):
        columns = slice(t * depth, (t + 1) * depth)
        out = keep_ref[:, columns] + a_ref[:block, columns].astype(F32)
        for low, half in ((me & bit_b, out.astype(BF16)), ((me & bit_b) ^ bit_b, b_ref[:, columns])):
            at = pl.multiple_of((low | (t * bit_a)) * depth, depth)
            out_ref[:, pl.ds(at, depth)] = half
    own, size = own_ref.shape[0], own_ref.shape[1]
    cols = own * size
    fold = a_ref.shape[1] // cols
    high = size // fold
    rows = heads_ref.shape[0] - size
    for h in range(own):
        final_ref[me * own + h] = own_ref[h]
        columns = slice(h * size, (h + 1) * size)
        at = (me ^ bit_b) * own + h
        final_ref[at] = resident_ref[at] + heads_ref[rows:, columns].astype(F32)
        for i, offset in enumerate((bit_a, bit_a | bit_b)):
            at = (me ^ offset) * own + h
            for q in range(fold):
                inner = slice(q * high, (q + 1) * high)
                change = a_ref[
                    block + i * high : block + (i + 1) * high,
                    q * cols + h * size : q * cols + (h + 1) * size,
                ]
                final_ref[at, inner, :] = resident_ref[at, inner, :] + change.astype(F32)


def last(info, count, keep, from_a, from_b, heads_b, resident, own_state):
    block, half = keep.shape
    return pl.pallas_call(
        functools.partial(last_kernel, count),
        out_shape=(
            jax.ShapeDtypeStruct((block, 2 * half), BF16),
            jax.ShapeDtypeStruct(resident.shape, F32),
        ),
        in_specs=[SMEM] + [VMEM] * 6,
        out_specs=(VMEM, VMEM),
        cost_estimate=pl.CostEstimate(
            flops=4 * block * half, bytes_accessed=4 << 20, transcendentals=0
        ),
        compiler_params=limit(9),
        name="last",
    )(info, keep, from_a, from_b, heads_b, resident, own_state)


def paired_body(
    section_inputs, fresh_group, resident_state, qkv_weight, out_weight, input_gain, head_gain
):
    count = lax.axis_size("row")
    sections = lax.axis_size("section")
    row, section = lax.axis_index("row"), lax.axis_index("section")
    place = jnp.where(section == 0, 2, jnp.where(section == sections - 1, 1, 0))
    info = (row + count * (place + 3 * (section % 2))).astype(jnp.int32)[None]
    x, resident, width = section_inputs[0], resident_state[0], input_gain.shape[1]

    own_half, other_half = halve(info, count, x)
    from_b = along(other_half, 1)
    from_a = along(own_half, 0)
    mine, partner, mine_b, partner_b = cut(info, qkv_weight[0], count)
    partner_b = along(partner_b, 0)
    from_far = along(from_b, 0)
    partner = along(partner, 0)
    out_own, out_other, fresh_own, fresh_other = halve(
        info, count, out_weight[0], fresh_group
    )
    outs_b = along(out_other, 1)
    fresh_partner = along(fresh_other, 1, sections - 1)
    given, scaled, rows, columns_b = given_product(
        info,
        count,
        input_gain,
        [own_half, from_a, from_b, from_far],
        [mine_b, partner_b],
    )
    got = along(given, 1)
    own, columns = own_product(info, count, scaled, [mine, partner])
    heads, own_state = attend(
        info, count, width, own, given, got, resident, head_gain
    )
    heads_b = along(heads, 1)
    pair = ([heads, heads_b], [out_own, outs_b])
    given_out = outgoing(info, count, *pair, mine=False)
    got_out = along(given_out, 0)
    own_out = outgoing(info, count, *pair, mine=True)
    next_mine, next_other = quarter(info, count, own_out, got_out, rows, fresh_own, fresh_partner)
    from_b = to_next(next_other, 0, 1)
    from_a = to_next(next_mine, 1, 0)
    own_half = to_next(next_mine, 0, 0)
    from_far = along(from_b, 0)
    given, scaled, rows = given_product(
        info, count, input_gain, [own_half, from_a, from_b, from_far], [columns_b]
    )
    got = along(given, 1)
    (own,) = own_product(info, count, scaled, [columns])
    heads, own_state = attend(info, count, width, own, given, got, own_state, head_gain, resident)
    heads_b = along(heads, 1)
    keep, to_a, to_b, cross = deal(
        info, count, [heads, heads_b], [out_own, outs_b], rows
    )
    cross = along(cross, 0)
    from_a = along(to_a, 0)
    to_b = combine(to_b, cross)
    from_b = along(to_b, 1)
    second_out, final_state = last(info, count, keep, from_a, from_b, heads_b, resident, own_state)
    return (second_out[None], final_state[None])


def solution(mesh):
    in_specs = (
        P("section", "row", None),
        P("row", None),
        P("section", None, None, None),
        P("section", "row", None),
        P("section", "row", None),
        P("section", None),
        P("section", None),
    )
    out_specs = (P("section", "row", None), P("section", None, None, None))

    def whole(*args):
        count = mesh.shape["row"]
        heads, size = args[2].shape[1:3]
        block = args[0].shape[1] // count
        paired = count == 4 and mesh.shape["section"] % 2 == 0 and heads % count == 0
        paired = paired and block * count <= 3 * heads // count * size
        body = paired_body if paired else gathered_body
        return jax.shard_map(
            body, mesh=mesh, in_specs=in_specs, out_specs=out_specs, check_vma=False
        )(*args)

    return whole
```

time: 288 us -> 121 us (0.42)
  waiting for transfers between devices: 240 us -> 82.1 us
  matrix products: 24 us -> 0 us
  starting transfers between devices: 1.77 us -> 23.8 us
  between operations: 14 us -> 0.83 us
  Pallas kernels: 0 us -> 11.8 us
  other arithmetic: 6.95 us -> 0 us
    all_gather x4 -> x0, waiting for transfers between devices: 237 us -> none  [the longest x1 126 us: body(): lax.all_gather(qkv_weight[0], 'row', axis=0, tiled=True)]
    ppermute x1 -> x19, waiting for transfers between devices: 1.48 us -> 82.1 us  [the longest x16 70.4 us: along(): return lax.ppermute(value, ('section', 'row'), pairs)]
    dot_general x10 -> x0, matrix products: 24 us -> none  [the longest x2 13.2 us: layer(): projected = jnp.dot(normed, qkv_full, preferred_element_type=jnp.float32)]
    ppermute x1 -> x19, starting transfers between devices: 1.61 us -> 23.8 us  [the longest x16 19.9 us: along(): return lax.ppermute(value, ('section', 'row'), pairs)]
    pallas_call x0 -> x15, Pallas kernels: none -> 11.8 us  [the longest x2 3.19 us: attend(): pl.pallas_call(functools.partial(attend_kernel, count, first, width), out...]
    reduce_sum x4 -> x0, other arithmetic: 4.98 us -> none  [the longest x2 3.47 us: layer(): total = jnp.sum(every, axis=0)]
  transfers between devices with their start and end apart: 5 -> 19, of which waited for: 5 -> 17; matrix products, arithmetic and copies ran while one was open for 1% -> 0% of each run, Pallas kernels for 0% -> 5%
where the time goes in v1:
time: 121 us; the launch traced here: 120 us
  waiting for transfers between devices  82.1 us (68%)
  starting transfers between devices  23.8 us (20%)
  Pallas kernels  11.8 us (10%)
  local copies, waits for them, and re-layouts  1.92 us (2%)
    ppermute x16, waiting for transfers between devices, along(): return lax.ppermute(value, ('section', 'row'), pairs)  70.4 us
    ppermute x16, starting transfers between devices, along(): return lax.ppermute(value, ('section', 'row'), pairs)  19.9 us
    ppermute x3, waiting for transfers between devices, to_next(): return lax.ppermute(value, ('section', 'row'), pairs)  11.7 us
    ppermute x3, starting transfers between devices, to_next(): return lax.ppermute(value, ('section', 'row'), pairs)  3.85 us
    pallas_call x2, Pallas kernels, attend(): pl.pallas_call(functools.partial(attend_kernel, count, first, width), out...  3.19 us
    pallas_call x2, Pallas kernels, given_product(): pl.pallas_call(functools.partial(given_kernel, count, first), out_shape=o...  2.77 us
  transfers between devices with their start and end apart: 19, of which 17 were waited for; matrix products, arithmetic and copies ran while one was open for 0% of the time, Pallas kernels for 5%

profile of v1, /device:TPU:0, one launch (start us, length us, event | category | flops | bytes accessed | tf_op | source)
XLA Modules:
  0.0 120.4 jit_solution(3202062883110566233)
XLA Ops:
  0.7 1.9 %copy-done.1 = bf16[1,512,3072]{2,1,0:T(8,128)(2,1)S(1)} copy-done((bf16[1,512,3072]{2,1,0:T(8,128)(2,1)S(1)}, bf16[1,512,3072]{2,1,0:T(8,128)(2,1)}, u32[]{:S(2)}) %copy-start.1) | copy-done | bytes 3145752
  3.0 3.0 %collective-permute-start.3 = (bf16[512,768]{1,0:T(8,128)(2,1)S(1)}, bf16[512,768]{1,0:T(8,128)(2,1)S(1)}, u32[]{:S(2)}, u32[]{:S(2)}) collective-permute-start(bf16[512,768]{1,0:T(8,128)(2,1)S(1)} %get-tuple-element.36), channel_id=1, source_target_pairs={{0,1},{1,0},{2,3},{3,2},{4,6},{5,7},{6,4},{7,5},{8,9},{9,8},{10,11... | collective-permute-start | bytes 2359304 | tf_op jit(solution)/shard_map/ppermute | solution.py:90
  6.1 1.6 %collective-permute-start.1 = (bf16[128,1024]{1,0:T(8,128)(2,1)S(1)}, bf16[128,1024]{1,0:T(8,128)(2,1)S(1)}, u32[]{:S(2)}, u32[]{:S(2)}) collective-permute-start(bf16[128,1024]{1,0:T(8,128)(2,1)S(1)} %get-tuple-element.34), channel_id=1, source_target_pairs={{0,2},{1,3},{2,0},{3,1},{4,5},{5,4},{6,7},{7,6},{8,10},{9,11},{10,... | collective-permute-start | bytes 786440 | tf_op jit(solution)/shard_map/ppermute | solution.py:90
  8.2 7.1 %collective-permute-done.1.refs_2_ = bf16[128,1024]{1,0:T(8,128)(2,1)S(1)} collective-permute-done((bf16[128,1024]{1,0:T(8,128)(2,1)S(1)}, bf16[128,1024]{1,0:T(8,128)(2,1)S(1)}, u32[]{:S(2)}, u32[]{:S(2)}) %collective-permute-start.1) | collective-permute-done | bytes 262176 | tf_op jit(solution)/shard_map/ppermute | solution.py:90
  15.9 1.5 %collective-permute-start.4 = (bf16[512,768]{1,0:T(8,128)(2,1)S(1)}, bf16[512,768]{1,0:T(8,128)(2,1)S(1)}, u32[]{:S(2)}, u32[]{:S(2)}) collective-permute-start(bf16[512,768]{1,0:T(8,128)(2,1)S(1)} %get-tuple-element.39), channel_id=1, source_target_pairs={{0,1},{1,0},{2,3},{3,2},{4,6},{5,7},{6,4},{7,5},{8,9},{9,8},{10,11... | collective-permute-start | bytes 2359304 | tf_op jit(solution)/shard_map/ppermute | solution.py:90
  17.3 4.2 %collective-permute-done.refs_1_ = bf16[128,1024]{1,0:T(8,128)(2,1)S(1)} collective-permute-done((bf16[128,1024]{1,0:T(8,128)(2,1)S(1)}, bf16[128,1024]{1,0:T(8,128)(2,1)S(1)}, u32[]{:S(2)}, u32[]{:S(2)}) %collective-permute-start) | collective-permute-done | bytes 262176 | tf_op jit(solution)/shard_map/ppermute | solution.py:90
  21.6 2.8 %collective-permute-done.2.refs_3_ = bf16[128,1024]{1,0:T(8,128)(2,1)S(1)} collective-permute-done((bf16[128,1024]{1,0:T(8,128)(2,1)S(1)}, bf16[128,1024]{1,0:T(8,128)(2,1)S(1)}, u32[]{:S(2)}, u32[]{:S(2)}) %collective-permute-start.2) | collective-permute-done | bytes 262176 | tf_op jit(solution)/shard_map/ppermute | solution.py:90
  24.4 1.4 %given_first.1 = (bf16[528,768]{1,0:T(8,128)(2,1)S(1)}, bf16[512,1024]{1,0:T(8,128)(2,1)S(1)}, bf16[512,1024]{1,0:T(8,128)(2,1)S(1)}, bf16[1024,768]{1,0:T(8,128)(2,1)S(1)}) custom-call(s32[1]{0:T(128)} %bitcast.info_ref, f32[1,2048]{1,0:T(1,128)S(1)} %copy-done.6, bf16[128,1024]{1,0:T(8,128)(2,1)S(1)} %get-tuple-element.33.refs_0_, ...), custom_call_target="tpu_custom_call" | custom-call | flops 805306368 | bytes 4194304 | tf_op jit(solution)/shard_map/given_first/pallas_call | solution.py:226
  25.8 1.7 %collective-permute-start.5 = (bf16[528,768]{1,0:T(8,128)(2,1)S(1)}, bf16[528,768]{1,0:T(8,128)(2,1)S(1)}, u32[]{:S(2)}, u32[]{:S(2)}) collective-permute-start(bf16[528,768]{1,0:T(8,128)(2,1)S(1)} %get-tuple-element.41.refs_1_), channel_id=1, source_target_pairs={{0,2},{1,3},{2,0},{3,1},{4,5},{5,4},{6,7},{7,6},{8,10},{9,11},{10,... | collective-permute-start | bytes 2433032 | tf_op jit(solution)/shard_map/ppermute | solution.py:90
  28.1 9.7 %collective-permute-done.4.refs_1_ = bf16[512,768]{1,0:T(8,128)(2,1)S(1)} collective-permute-done((bf16[512,768]{1,0:T(8,128)(2,1)S(1)}, bf16[512,768]{1,0:T(8,128)(2,1)S(1)}, u32[]{:S(2)}, u32[]{:S(2)}) %collective-permute-start.4) | collective-permute-done | bytes 786464 | tf_op jit(solution)/shard_map/ppermute | solution.py:90
  37.9 1.1 own_first.1
  39.0 1.7 %collective-permute-done.5.refs_2_ = bf16[528,768]{1,0:T(8,128)(2,1)S(1)} collective-permute-done((bf16[528,768]{1,0:T(8,128)(2,1)S(1)}, bf16[528,768]{1,0:T(8,128)(2,1)S(1)}, u32[]{:S(2)}, u32[]{:S(2)}) %collective-permute-start.5) | collective-permute-done | bytes 811040 | tf_op jit(solution)/shard_map/ppermute | solution.py:90
  40.7 1.6 %attend_first.1 = (bf16[512,256]{1,0:T(8,128)(2,1)S(1)}, f32[2,128,128]{2,1,0:T(8,128)S(1)}) custom-call(s32[1]{0:T(128)} %bitcast.info_ref, f32[512,768]{1,0:T(8,128)S(1)} %get-tuple-element.40.refs_0_, bf16[528,768]{1,0:T(8,128)(2,1)S(1)} %get-tuple-element.41.refs_1_, bf16[528,768]{1,0:T(8,128)(2,1)S(1)} %collective-permute-done.5.refs_2_, ...), custom_call_target="tpu_custom_call" | custom-call | flops 167772160 | bytes 8388608 | tf_op jit(solution)/shard_map/attend_first/pallas_call | solution.py:338
  42.3 1.8 %collective-permute-start.6 = (bf16[512,256]{1,0:T(8,128)(2,1)S(1)}, bf16[512,256]{1,0:T(8,128)(2,1)S(1)}, u32[]{:S(2)}, u32[]{:S(2)}) collective-permute-start(bf16[512,256]{1,0:T(8,128)(2,1)S(1)} %get-tuple-element.42.refs_0_), channel_id=1, source_target_pairs={{0,2},{1,3},{2,0},{3,1},{4,5},{5,4},{6,7},{7,6},{8,10},{9,11},{10,... | collective-permute-start | bytes 786440 | tf_op jit(solution)/shard_map/ppermute | solution.py:90
  44.1 2.2 %collective-permute-done.7.refs_3_ = bf16[256,1024]{1,0:T(8,128)(2,1)S(1)} collective-permute-done((bf16[256,1024]{1,0:T(8,128)(2,1)S(1)}, bf16[256,1024]{1,0:T(8,128)(2,1)S(1)}, u32[]{:S(2)}, u32[]{:S(2)}) %collective-permute-start.7) | collective-permute-done | bytes 524320 | tf_op jit(solution)/shard_map/ppermute | solution.py:90
  46.3 2.8 %collective-permute-done.6.refs_1_ = bf16[512,256]{1,0:T(8,128)(2,1)S(1)} collective-permute-done((bf16[512,256]{1,0:T(8,128)(2,1)S(1)}, bf16[512,256]{1,0:T(8,128)(2,1)S(1)}, u32[]{:S(2)}, u32[]{:S(2)}) %collective-permute-start.6) | collective-permute-done | bytes 262176 | tf_op jit(solution)/shard_map/ppermute | solution.py:90
  49.5 1.8 %collective-permute-start.8 = (bf16[256,1024]{1,0:T(8,128)(2,1)S(1)}, bf16[256,1024]{1,0:T(8,128)(2,1)S(1)}, u32[]{:S(2)}, u32[]{:S(2)}) collective-permute-start(bf16[256,1024]{1,0:T(8,128)(2,1)S(1)} %outgoing_given.1), channel_id=1, source_target_pairs={{0,1},{1,0},{2,3},{3,2},{4,6},{5,7},{6,4},{7,5},{8,9},{9,8},{10,11... | collective-permute-start | bytes 1572872 | tf_op jit(solution)/shard_map/ppermute | solution.py:90
  52.4 6.3 %collective-permute-done.8.got_ref = bf16[256,1024]{1,0:T(8,128)(2,1)S(1)} collective-permute-done((bf16[256,1024]{1,0:T(8,128)(2,1)S(1)}, bf16[256,1024]{1,0:T(8,128)(2,1)S(1)}, u32[]{:S(2)}, u32[]{:S(2)}) %collective-permute-start.8) | collective-permute-done | bytes 524320 | tf_op jit(solution)/shard_map/ppermute | solution.py:90
  59.0 1.5 %collective-permute-start.12 = (bf16[256,512]{1,0:T(8,128)(2,1)S(1)}, bf16[256,512]{1,0:T(8,128)(2,1)S(1)}, u32[]{:S(2)}, u32[]{:S(2)}) collective-permute-start(bf16[256,512]{1,0:T(8,128)(2,1)S(1)} %get-tuple-element.49), channel_id=1, source_target_pairs={{0,5},{1,4},{2,7},{3,6},{4,10},{5,11},{6,8},{7,9},{8,13},{9,12},{1... | collective-permute-start | bytes 786440 | tf_op jit(solution)/shard_map/ppermute | solution.py:100
  60.5 1.5 %collective-permute-start.10 = (bf16[256,512]{1,0:T(8,128)(2,1)S(1)}, bf16[256,512]{1,0:T(8,128)(2,1)S(1)}, u32[]{:S(2)}, u32[]{:S(2)}) collective-permute-start(bf16[256,512]{1,0:T(8,128)(2,1)S(1)} %get-tuple-element.48), channel_id=1, source_target_pairs={{0,4},{1,5},{2,6},{3,7},{4,8},{5,9},{6,10},{7,11},{8,12},{9,13},{1... | collective-permute-start | bytes 786440 | tf_op jit(solution)/shard_map/ppermute | solution.py:100
  62.9 7.0 %collective-permute-done.12.refs_2_ = bf16[256,512]{1,0:T(8,128)(2,1)S(1)} collective-permute-done((bf16[256,512]{1,0:T(8,128)(2,1)S(1)}, bf16[256,512]{1,0:T(8,128)(2,1)S(1)}, u32[]{:S(2)}, u32[]{:S(2)}) %collective-permute-start.12) | collective-permute-done | bytes 262176 | tf_op jit(solution)/shard_map/ppermute | solution.py:100
  69.9 1.5 %collective-permute-start.13 = (bf16[256,512]{1,0:T(8,128)(2,1)S(1)}, bf16[256,512]{1,0:T(8,128)(2,1)S(1)}, u32[]{:S(2)}, u32[]{:S(2)}) collective-permute-start(bf16[256,512]{1,0:T(8,128)(2,1)S(1)} %collective-permute-done.12.refs_2_), channel_id=1, source_target_pairs={{0,1},{1,0},{2,3},{3,2},{4,6},{5,7},{6,4},{7,5},{8,9},{9,8},{10,11... | collective-permute-start | bytes 786440 | tf_op jit(solution)/shard_map/ppermute | solution.py:90
  72.3 3.8 %collective-permute-done.11.refs_1_ = bf16[256,512]{1,0:T(8,128)(2,1)S(1)} collective-permute-done((bf16[256,512]{1,0:T(8,128)(2,1)S(1)}, bf16[256,512]{1,0:T(8,128)(2,1)S(1)}, u32[]{:S(2)}, u32[]{:S(2)}) %collective-permute-start.11) | collective-permute-done | bytes 262176 | tf_op jit(solution)/shard_map/ppermute | solution.py:100
  76.1 3.6 %collective-permute-done.13.refs_3_ = bf16[256,512]{1,0:T(8,128)(2,1)S(1)} collective-permute-done((bf16[256,512]{1,0:T(8,128)(2,1)S(1)}, bf16[256,512]{1,0:T(8,128)(2,1)S(1)}, u32[]{:S(2)}, u32[]{:S(2)}) %collective-permute-start.13) | collective-permute-done | bytes 262176 | tf_op jit(solution)/shard_map/ppermute | solution.py:90
  79.7 1.4 %given_second.1 = (bf16[528,768]{1,0:T(8,128)(2,1)S(1)}, bf16[512,1024]{1,0:T(8,128)(2,1)S(1)}, bf16[512,1024]{1,0:T(8,128)(2,1)S(1)}) custom-call(s32[1]{0:T(128)} %bitcast.info_ref, f32[1,2048]{1,0:T(1,128)S(1)} %copy-done.6, bf16[256,512]{1,0:T(8,128)(2,1)S(1)} %collective-permute-done.10.refs_0_, bf16[256,512]{1,0:T(8,128)(2,1)S(1)} %collective-permute-done.11.refs_1_, ...), custom_call_target="tpu_custom_call" | custom-call | flops 805306368 | bytes 4194304 | tf_op jit(solution)/shard_map/given_second/pallas_call | solution.py:226
  82.9 10.5 %collective-permute-done.14.refs_2_ = bf16[528,768]{1,0:T(8,128)(2,1)S(1)} collective-permute-done((bf16[528,768]{1,0:T(8,128)(2,1)S(1)}, bf16[528,768]{1,0:T(8,128)(2,1)S(1)}, u32[]{:S(2)}, u32[]{:S(2)}) %collective-permute-start.14) | collective-permute-done | bytes 811040 | tf_op jit(solution)/shard_map/ppermute | solution.py:90
  93.3 1.6 %attend_second.1 = (bf16[640,256]{1,0:T(8,128)(2,1)S(1)}, f32[2,128,128]{2,1,0:T(8,128)S(1)}) custom-call(s32[1]{0:T(128)} %bitcast.info_ref, f32[512,768]{1,0:T(8,128)S(1)} %own_second.1.refs_0_, bf16[528,768]{1,0:T(8,128)(2,1)S(1)} %get-tuple-element.53.refs_1_, bf16[528,768]{1,0:T(8,128)(2,1)S(1)} %collective-permute-done.14.refs_2_, ...), custom_call_target="tpu_custom_call" | custom-call | flops 167772160 | bytes 8388608 | tf_op jit(solution)/shard_map/attend_second/pallas_call | solution.py:338
  95.8 9.6 %collective-permute-done.15.refs_1_.heads_ref = bf16[640,256]{1,0:T(8,128)(2,1)S(1)} collective-permute-done((bf16[640,256]{1,0:T(8,128)(2,1)S(1)}, bf16[640,256]{1,0:T(8,128)(2,1)S(1)}, u32[]{:S(2)}, u32[]{:S(2)}) %collective-permute-start.15) | collective-permute-done | bytes 327712 | tf_op jit(solution)/shard_map/ppermute | solution.py:90
  106.4 2.0 %collective-permute-start.16 = (bf16[192,1024]{1,0:T(8,128)(2,1)S(1)}, bf16[192,1024]{1,0:T(8,128)(2,1)S(1)}, u32[]{:S(2)}, u32[]{:S(2)}) collective-permute-start(bf16[192,1024]{1,0:T(8,128)(2,1)S(1)} %get-tuple-element.58), channel_id=1, source_target_pairs={{0,1},{1,0},{2,3},{3,2},{4,6},{5,7},{6,4},{7,5},{8,9},{9,8},{10,11... | collective-permute-start | bytes 1179656 | tf_op jit(solution)/shard_map/ppermute | solution.py:90
  108.4 4.4 %collective-permute-done.17.got_ref = bf16[128,1024]{1,0:T(8,128)(2,1)S(1)} collective-permute-done((bf16[128,1024]{1,0:T(8,128)(2,1)S(1)}, bf16[128,1024]{1,0:T(8,128)(2,1)S(1)}, u32[]{:S(2)}, u32[]{:S(2)}) %collective-permute-start.17) | collective-permute-done | bytes 262176 | tf_op jit(solution)/shard_map/ppermute | solution.py:90
  113.9 3.1 %collective-permute-done.16.a_ref = bf16[192,1024]{1,0:T(8,128)(2,1)S(1)} collective-permute-done((bf16[192,1024]{1,0:T(8,128)(2,1)S(1)}, bf16[192,1024]{1,0:T(8,128)(2,1)S(1)}, u32[]{:S(2)}, u32[]{:S(2)}) %collective-permute-start.16) | collective-permute-done | bytes 393248 | tf_op jit(solution)/shard_map/ppermute | solution.py:90
  117.0 2.3 %collective-permute-done.18.b_ref = bf16[128,1024]{1,0:T(8,128)(2,1)S(1)} collective-permute-done((bf16[128,1024]{1,0:T(8,128)(2,1)S(1)}, bf16[128,1024]{1,0:T(8,128)(2,1)S(1)}, u32[]{:S(2)}, u32[]{:S(2)}) %collective-permute-start.18) | collective-permute-done | bytes 262176 | tf_op jit(solution)/shard_map/ppermute | solution.py:90
  (35 shorter events, 11.6 us)
Async XLA Ops:
  0.7 1.9 %copy-start.1 = (bf16[1,512,3072]{2,1,0:T(8,128)(2,1)S(1)}, bf16[1,512,3072]{2,1,0:T(8,128)(2,1)}, u32[]{:S(2)}) copy-start(bf16[1,512,3072]{2,1,0:T(8,128)(2,1)} %param.10) | copy-start | bytes 9437188
  2.5 3.4 %copy-start.3 = (bf16[1,128,2048]{2,1,0:T(8,128)(2,1)S(1)}, bf16[1,128,2048]{2,1,0:T(8,128)(2,1)}, u32[]{:S(2)}) copy-start(bf16[1,128,2048]{2,1,0:T(8,128)(2,1)} %param.7) | copy-start | bytes 1572868
  2.5 21.8 %copy-start.6 = (f32[1,2048]{1,0:T(1,128)S(1)}, f32[1,2048]{1,0:T(1,128)}, u32[]{:S(2)}) copy-start(f32[1,2048]{1,0:T(1,128)} %gain_ref.3) | copy-start | bytes 24580
  3.0 21.4 %collective-permute-start.3 = (bf16[512,768]{1,0:T(8,128)(2,1)S(1)}, bf16[512,768]{1,0:T(8,128)(2,1)S(1)}, u32[]{:S(2)}, u32[]{:S(2)}) collective-permute-start(bf16[512,768]{1,0:T(8,128)(2,1)S(1)} %get-tuple-element.36), channel_id=1, source_target_pairs={{0,1},{1,0},{2,3},{3,2},{4,6},{5,7},{6,4},{7,5},{8,9},{9,8},{10,11... | collective-permute-start | bytes 2359304 | tf_op jit(solution)/shard_map/ppermute | solution.py:90
  6.0 21.4 %copy-start.2 = (bf16[1,256,2048]{2,1,0:T(8,128)(2,1)S(1)}, bf16[1,256,2048]{2,1,0:T(8,128)(2,1)}, u32[]{:S(2)}) copy-start(bf16[1,256,2048]{2,1,0:T(8,128)(2,1)} %param.11) | copy-start | bytes 3145732
  6.0 21.4 %copy-start.4 = (bf16[128,2048]{1,0:T(8,128)(2,1)S(1)}, bf16[128,2048]{1,0:T(8,128)(2,1)}, u32[]{:S(2)}) copy-start(bf16[128,2048]{1,0:T(8,128)(2,1)} %refs_1_.1) | copy-start | bytes 1572868
  6.1 9.2 %collective-permute-start.1 = (bf16[128,1024]{1,0:T(8,128)(2,1)S(1)}, bf16[128,1024]{1,0:T(8,128)(2,1)S(1)}, u32[]{:S(2)}, u32[]{:S(2)}) collective-permute-start(bf16[128,1024]{1,0:T(8,128)(2,1)S(1)} %get-tuple-element.34), channel_id=1, source_target_pairs={{0,2},{1,3},{2,0},{3,1},{4,5},{5,4},{6,7},{7,6},{8,10},{9,11},{10,... | collective-permute-start | bytes 786440 | tf_op jit(solution)/shard_map/ppermute | solution.py:90
  7.6 13.9 %collective-permute-start = (bf16[128,1024]{1,0:T(8,128)(2,1)S(1)}, bf16[128,1024]{1,0:T(8,128)(2,1)S(1)}, u32[]{:S(2)}, u32[]{:S(2)}) collective-permute-start(bf16[128,1024]{1,0:T(8,128)(2,1)S(1)} %get-tuple-element.33.refs_0_), channel_id=1, source_target_pairs={{0,1},{1,0},{2,3},{3,2},{4,6},{5,7},{6,4},{7,5},{8,9},{9,8},{10,11... | collective-permute-start | bytes 786440 | tf_op jit(solution)/shard_map/ppermute | solution.py:90
  15.3 9.1 %collective-permute-start.2 = (bf16[128,1024]{1,0:T(8,128)(2,1)S(1)}, bf16[128,1024]{1,0:T(8,128)(2,1)S(1)}, u32[]{:S(2)}, u32[]{:S(2)}) collective-permute-start(bf16[128,1024]{1,0:T(8,128)(2,1)S(1)} %collective-permute-done.1.refs_2_), channel_id=1, source_target_pairs={{0,1},{1,0},{2,3},{3,2},{4,6},{5,7},{6,4},{7,5},{8,9},{9,8},{10,11... | collective-permute-start | bytes 786440 | tf_op jit(solution)/shard_map/ppermute | solution.py:90
  15.9 22.0 %collective-permute-start.4 = (bf16[512,768]{1,0:T(8,128)(2,1)S(1)}, bf16[512,768]{1,0:T(8,128)(2,1)S(1)}, u32[]{:S(2)}, u32[]{:S(2)}) collective-permute-start(bf16[512,768]{1,0:T(8,128)(2,1)S(1)} %get-tuple-element.39), channel_id=1, source_target_pairs={{0,1},{1,0},{2,3},{3,2},{4,6},{5,7},{6,4},{7,5},{8,9},{9,8},{10,11... | collective-permute-start | bytes 2359304 | tf_op jit(solution)/shard_map/ppermute | solution.py:90
  25.8 14.9 %collective-permute-start.5 = (bf16[528,768]{1,0:T(8,128)(2,1)S(1)}, bf16[528,768]{1,0:T(8,128)(2,1)S(1)}, u32[]{:S(2)}, u32[]{:S(2)}) collective-permute-start(bf16[528,768]{1,0:T(8,128)(2,1)S(1)} %get-tuple-element.41.refs_1_), channel_id=1, source_target_pairs={{0,2},{1,3},{2,0},{3,1},{4,5},{5,4},{6,7},{7,6},{8,10},{9,11},{10,... | collective-permute-start | bytes 2433032 | tf_op jit(solution)/shard_map/ppermute | solution.py:90
  27.6 13.1 %copy-start = (f32[1,8,128,128]{3,2,1,0:T(8,128)S(1)}, f32[1,8,128,128]{3,2,1,0:T(8,128)}, u32[]{:S(2)}) copy-start(f32[1,8,128,128]{3,2,1,0:T(8,128)} %param.9) | copy-start | bytes 1572868
  27.6 13.0 %copy-start.5 = (f32[1,1024]{1,0:T(1,128)S(1)}, f32[1,1024]{1,0:T(1,128)}, u32[]{:S(2)}) copy-start(f32[1,1024]{1,0:T(1,128)} %refs_4_.3) | copy-start | bytes 12292
  27.6 18.6 %collective-permute-start.7 = (bf16[256,1024]{1,0:T(8,128)(2,1)S(1)}, bf16[256,1024]{1,0:T(8,128)(2,1)S(1)}, u32[]{:S(2)}, u32[]{:S(2)}) collective-permute-start(bf16[256,1024]{1,0:T(8,128)(2,1)S(1)} %get-tuple-element.44), channel_id=1, source_target_pairs={{0,2},{1,3},{2,0},{3,1},{4,5},{5,4},{6,7},{7,6},{8,10},{9,11},{10,... | collective-permute-start | bytes 1572872 | tf_op jit(solution)/shard_map/ppermute | solution.py:90
  42.3 6.8 %collective-permute-start.6 = (bf16[512,256]{1,0:T(8,128)(2,1)S(1)}, bf16[512,256]{1,0:T(8,128)(2,1)S(1)}, u32[]{:S(2)}, u32[]{:S(2)}) collective-permute-start(bf16[512,256]{1,0:T(8,128)(2,1)S(1)} %get-tuple-element.42.refs_0_), channel_id=1, source_target_pairs={{0,2},{1,3},{2,0},{3,1},{4,5},{5,4},{6,7},{7,6},{8,10},{9,11},{10,... | collective-permute-start | bytes 786440 | tf_op jit(solution)/shard_map/ppermute | solution.py:90
  49.5 9.2 %collective-permute-start.8 = (bf16[256,1024]{1,0:T(8,128)(2,1)S(1)}, bf16[256,1024]{1,0:T(8,128)(2,1)S(1)}, u32[]{:S(2)}, u32[]{:S(2)}) collective-permute-start(bf16[256,1024]{1,0:T(8,128)(2,1)S(1)} %outgoing_given.1), channel_id=1, source_target_pairs={{0,1},{1,0},{2,3},{3,2},{4,6},{5,7},{6,4},{7,5},{8,9},{9,8},{10,11... | collective-permute-start | bytes 1572872 | tf_op jit(solution)/shard_map/ppermute | solution.py:90
  51.3 1.1 collective-permute-start.9
  59.0 10.8 %collective-permute-start.12 = (bf16[256,512]{1,0:T(8,128)(2,1)S(1)}, bf16[256,512]{1,0:T(8,128)(2,1)S(1)}, u32[]{:S(2)}, u32[]{:S(2)}) collective-permute-start(bf16[256,512]{1,0:T(8,128)(2,1)S(1)} %get-tuple-element.49), channel_id=1, source_target_pairs={{0,5},{1,4},{2,7},{3,6},{4,10},{5,11},{6,8},{7,9},{8,13},{9,12},{1... | collective-permute-start | bytes 786440 | tf_op jit(solution)/shard_map/ppermute | solution.py:100
  60.5 11.7 %collective-permute-start.10 = (bf16[256,512]{1,0:T(8,128)(2,1)S(1)}, bf16[256,512]{1,0:T(8,128)(2,1)S(1)}, u32[]{:S(2)}, u32[]{:S(2)}) collective-permute-start(bf16[256,512]{1,0:T(8,128)(2,1)S(1)} %get-tuple-element.48), channel_id=1, source_target_pairs={{0,4},{1,5},{2,6},{3,7},{4,8},{5,9},{6,10},{7,11},{8,12},{9,13},{1... | collective-permute-start | bytes 786440 | tf_op jit(solution)/shard_map/ppermute | solution.py:100
  62.0 14.1 %collective-permute-start.11 = (bf16[256,512]{1,0:T(8,128)(2,1)S(1)}, bf16[256,512]{1,0:T(8,128)(2,1)S(1)}, u32[]{:S(2)}, u32[]{:S(2)}) collective-permute-start(bf16[256,512]{1,0:T(8,128)(2,1)S(1)} %get-tuple-element.48), channel_id=1, source_target_pairs={{0,6},{1,7},{2,4},{3,5},{4,9},{5,8},{6,11},{7,10},{8,14},{9,15},{1... | collective-permute-start | bytes 786440 | tf_op jit(solution)/shard_map/ppermute | solution.py:100
  69.9 9.8 %collective-permute-start.13 = (bf16[256,512]{1,0:T(8,128)(2,1)S(1)}, bf16[256,512]{1,0:T(8,128)(2,1)S(1)}, u32[]{:S(2)}, u32[]{:S(2)}) collective-permute-start(bf16[256,512]{1,0:T(8,128)(2,1)S(1)} %collective-permute-done.12.refs_2_), channel_id=1, source_target_pairs={{0,1},{1,0},{2,3},{3,2},{4,6},{5,7},{6,4},{7,5},{8,9},{9,8},{10,11... | collective-permute-start | bytes 786440 | tf_op jit(solution)/shard_map/ppermute | solution.py:90
  81.0 12.3 %collective-permute-start.14 = (bf16[528,768]{1,0:T(8,128)(2,1)S(1)}, bf16[528,768]{1,0:T(8,128)(2,1)S(1)}, u32[]{:S(2)}, u32[]{:S(2)}) collective-permute-start(bf16[528,768]{1,0:T(8,128)(2,1)S(1)} %get-tuple-element.53.refs_1_), channel_id=1, source_target_pairs={{0,2},{1,3},{2,0},{3,1},{4,5},{5,4},{6,7},{7,6},{8,10},{9,11},{10,... | collective-permute-start | bytes 2433032 | tf_op jit(solution)/shard_map/ppermute | solution.py:90
  94.9 10.5 %collective-permute-start.15 = (bf16[640,256]{1,0:T(8,128)(2,1)S(1)}, bf16[640,256]{1,0:T(8,128)(2,1)S(1)}, u32[]{:S(2)}, u32[]{:S(2)}) collective-permute-start(bf16[640,256]{1,0:T(8,128)(2,1)S(1)} %get-tuple-element.55.refs_0_), channel_id=1, source_target_pairs={{0,2},{1,3},{2,0},{3,1},{4,5},{5,4},{6,7},{7,6},{8,10},{9,11},{10,... | collective-permute-start | bytes 983048 | tf_op jit(solution)/shard_map/ppermute | solution.py:90
  106.3 6.5 %collective-permute-start.17 = (bf16[128,1024]{1,0:T(8,128)(2,1)S(1)}, bf16[128,1024]{1,0:T(8,128)(2,1)S(1)}, u32[]{:S(2)}, u32[]{:S(2)}) collective-permute-start(bf16[128,1024]{1,0:T(8,128)(2,1)S(1)} %get-tuple-element.60), channel_id=1, source_target_pairs={{0,1},{1,0},{2,3},{3,2},{4,6},{5,7},{6,4},{7,5},{8,9},{9,8},{10,11... | collective-permute-start | bytes 786440 | tf_op jit(solution)/shard_map/ppermute | solution.py:90
  106.4 10.6 %collective-permute-start.16 = (bf16[192,1024]{1,0:T(8,128)(2,1)S(1)}, bf16[192,1024]{1,0:T(8,128)(2,1)S(1)}, u32[]{:S(2)}, u32[]{:S(2)}) collective-permute-start(bf16[192,1024]{1,0:T(8,128)(2,1)S(1)} %get-tuple-element.58), channel_id=1, source_target_pairs={{0,1},{1,0},{2,3},{3,2},{4,6},{5,7},{6,4},{7,5},{8,9},{9,8},{10,11... | collective-permute-start | bytes 1179656 | tf_op jit(solution)/shard_map/ppermute | solution.py:90
  112.9 6.4 %collective-permute-start.18 = (bf16[128,1024]{1,0:T(8,128)(2,1)S(1)}, bf16[128,1024]{1,0:T(8,128)(2,1)S(1)}, u32[]{:S(2)}, u32[]{:S(2)}) collective-permute-start(bf16[128,1024]{1,0:T(8,128)(2,1)S(1)} %combine.1), channel_id=1, source_target_pairs={{0,2},{1,3},{2,0},{3,1},{4,5},{5,4},{6,7},{7,6},{8,10},{9,11},{10,... | collective-permute-start | bytes 786440 | tf_op jit(solution)/shard_map/ppermute | solution.py:90

commit v2 on v1

--- a/solution.py
+++ b/solution.py
@@ -269,8 +269,8 @@
     own_ref, given_ref, got_ref, state_ref, gain_ref, refs = *refs[:5], refs[5:]
     if not first:
         resident_ref, refs = refs[0], refs[1:]
-    ho_ref, new_state_ref, qkv = refs
-    me, _, _, _ = whereabouts(info_ref, count)
+    other_ref, mine_ref, new_state_ref, qkv, ho_all = refs
+    me, _, bit_a, bit_b = whereabouts(info_ref, count)
     own, size = new_state_ref.shape[0], new_state_ref.shape[1]
     cols = own * size
     block = own_ref.shape[0] // count
@@ -315,14 +315,18 @@
             )
             mean = jnp.mean(attended * attended, axis=-1, keepdims=True)
             scaled = attended * lax.rsqrt(mean + 1e-06) * gains[:, h * size : (h + 1) * size]
-            ho_ref[rows, h * size : (h + 1) * size] = scaled.astype(BF16)
+            ho_all[rows, h * size : (h + 1) * size] = scaled.astype(BF16)
             prefix = prefix + lax.dot_general(
                 k, v, (((0,), (0,)), ((), ())), preferred_element_type=F32
             )
         new_state_ref[h] = prefix
         if not first:
             change = (prefix - resident_ref[me * own + h]).astype(BF16)
-            ho_ref[count * block :, h * size : (h + 1) * size] = change
+            mine_ref[2 * block :, h * size : (h + 1) * size] = change
+    for ref, low in ((other_ref, (me & bit_a) ^ bit_a), (mine_ref, me & bit_a)):
+        for t in range(2):
+            at = pl.multiple_of((low | (t * bit_b)) * block, block)
+            ref[t * block : (t + 1) * block, :] = ho_all[pl.ds(at, block), :]
 
 
 def attend(info, count, width, own, given, got, state, head_gain, resident=None):
@@ -332,7 +336,8 @@
     heads = cols3 // 3 // size
     ins = [info, own, given, got, state, head_gain] + ([] if first else [resident])
     outs = [
-        jax.ShapeDtypeStruct((rows + (0 if first else size), heads * size), BF16),
+        jax.ShapeDtypeStruct((rows // 2, heads * size), BF16),
+        jax.ShapeDtypeStruct((rows // 2 + (0 if first else size), heads * size), BF16),
         jax.ShapeDtypeStruct((heads, size, size), F32),
     ]
     return pl.pallas_call(
@@ -340,7 +345,10 @@
         out_shape=outs,
         in_specs=[SMEM] + [VMEM] * (len(ins) - 1),
         out_specs=[VMEM] * len(outs),
-        scratch_shapes=[pltpu.VMEM((rows, cols3), BF16)],
+        scratch_shapes=[
+            pltpu.VMEM((rows, cols3), BF16),
+            pltpu.VMEM((rows, heads * size), BF16),
+        ],
         cost_estimate=pl.CostEstimate(
             flops=10 * rows * heads * size * size, bytes_accessed=8 << 20, transcendentals=0
         ),
@@ -349,41 +357,33 @@
     )(*ins)
 
 
-def outgoing_kernel(count, mine, info_ref, *refs):
-    ho_refs, w_refs, out_ref, lhs = refs[:2], refs[2:4], refs[4], refs[5]
-    me, _, bit_a, bit_b = whereabouts(info_ref, count)
-    low = me & bit_a if mine else (me & bit_a) ^ bit_a
-    block, depth = ho_refs[0].shape[0] // count, ho_refs[0].shape[1]
-    for t in range(2):
-        at = pl.multiple_of((low | (t * bit_b)) * block, block)
-        for i, ho_ref in enumerate(ho_refs):
-            lhs[t * block : (t + 1) * block, i * depth : (i + 1) * depth] = ho_ref[
-                pl.ds(at, block), :
-            ]
+def product_of(ho_refs, w_refs, rows):
     total = None
-    for i, w_ref in enumerate(w_refs):
-        term = jnp.dot(
-            lhs[:, i * depth : (i + 1) * depth], w_ref[...], preferred_element_type=F32
-        )
+    for ho_ref, w_ref in zip(ho_refs, w_refs):
+        term = jnp.dot(ho_ref[rows, :], w_ref[...], preferred_element_type=F32)
         total = term if total is None else total + term
-    out_ref[...] = total.astype(out_ref.dtype)
-
-
-def outgoing(info, count, heads, weights, mine):
-    rows, depth = heads[0].shape[0] // 2, heads[0].shape[1]
+    return total
+
+
+def outgoing_kernel(*refs):
+    out_ref = refs[4]
+    out_ref[...] = product_of(refs[:2], refs[2:4], slice(None)).astype(out_ref.dtype)
+
+
+def outgoing(heads, weights, dtype):
+    rows, depth = heads[0].shape
     cols = weights[0].shape[1]
     return pl.pallas_call(
-        functools.partial(outgoing_kernel, count, mine),
-        out_shape=jax.ShapeDtypeStruct((rows, cols), F32 if mine else BF16),
-        in_specs=[SMEM] + [VMEM] * 4,
+        outgoing_kernel,
+        out_shape=jax.ShapeDtypeStruct((rows, cols), dtype),
+        in_specs=[VMEM] * 4,
         out_specs=VMEM,
-        scratch_shapes=[pltpu.VMEM((rows, 2 * depth), BF16)],
         cost_estimate=pl.CostEstimate(
             flops=4 * rows * depth * cols, bytes_accessed=4 << 20, transcendentals=0
         ),
         compiler_params=limit(9),
-        name="outgoing_mine" if mine else "outgoing_given",
-    )(info, *heads, *weights)
+        name="outgoing",
+    )(*heads, *weights)
 
 
 def quarter_kernel(count, info_ref, own_ref, got_ref, x_ref, fresh_ref, partner_ref, *refs):
@@ -426,56 +426,72 @@
     )(info, own, got, x, fresh, fresh_partner)
 
 
+def cross_kernel(count, info_ref, *refs):
+    out_ref = refs[4]
+    me, _, _, bit_b = whereabouts(info_ref, count)
+    block = out_ref.shape[0]
+    there = pl.multiple_of((1 - (me & bit_b) // bit_b) * block, block)
+    out_ref[...] = product_of(refs[:2], refs[2:4], pl.ds(there, block)).astype(BF16)
+
+
+def crossing(info, count, heads, weights):
+    return pl.pallas_call(
+        functools.partial(cross_kernel, count),
+        out_shape=jax.ShapeDtypeStruct((heads[0].shape[0] // 2, weights[0].shape[1]), BF16),
+        in_specs=[SMEM] + [VMEM] * 4,
+        out_specs=VMEM,
+        cost_estimate=pl.CostEstimate(
+            flops=2 * heads[0].size * weights[0].shape[1],
+            bytes_accessed=4 << 20,
+            transcendentals=0,
+        ),
+        compiler_params=limit(9),
+        name="crossing",
+    )(info, *heads, *weights)
+
+
 def deal_kernel(count, info_ref, *refs):
-    ho_refs, w_refs, x_ref, refs = refs[:2], refs[2:4], refs[4], refs[5:]
-    keep_ref, a_ref, b_ref, cross_ref, product = refs
-    me, _, bit_a, bit_b = whereabouts(info_ref, count)
-    rows, block = x_ref.shape[0], keep_ref.shape[0]
-    total = None
-    for ho_ref, w_ref in zip(ho_refs, w_refs):
-        term = jnp.dot(ho_ref[:rows, :], w_ref[...], preferred_element_type=F32)
-        total = term if total is None else total + term
-    product[...] = total
-    for out_ref, offset, residual in (
-        (cross_ref, bit_a | bit_b, False),
-        (a_ref, bit_a, False),
-        (b_ref, bit_b, True),
-        (keep_ref, 0, True),
-    ):
-        at = pl.ds(pl.multiple_of((me ^ offset) * block, block), block)
-        out = product[at, :]
-        if residual:
-            out = out + x_ref[at, :].astype(F32)
-        out_ref[:block, :] = out.astype(out_ref.dtype)
-    size, cols = ho_refs[0].shape[0] - rows, ho_refs[0].shape[1]
+    other_refs, mine_refs, w_refs, x_ref = refs[:2], refs[2:4], refs[4:6], refs[6]
+    keep_ref, a_ref, b_ref = refs[7:]
+    me, _, _, bit_b = whereabouts(info_ref, count)
+    block = keep_ref.shape[0]
+    second = (me & bit_b) // bit_b
+    for out_ref, part, offset in ((b_ref, 1 - second, bit_b), (keep_ref, second, 0)):
+        at = pl.multiple_of((me ^ offset) * block, block)
+        there = pl.ds(pl.multiple_of(part * block, block), block)
+        out_ref[...] = product_of(mine_refs, w_refs, there) + x_ref[
+            pl.ds(at, block), :
+        ].astype(F32)
+    here = pl.ds(pl.multiple_of(second * block, block), block)
+    a_ref[:block, :] = product_of(other_refs, w_refs, here).astype(BF16)
+    rows = 2 * block
+    size, cols = mine_refs[0].shape[0] - rows, mine_refs[0].shape[1]
     fold = x_ref.shape[1] // cols
     high = size // fold
-    for i, ho_ref in enumerate(ho_refs):
+    for i, ref in enumerate(mine_refs):
         for q in range(fold):
-            a_ref[block + i * high : block + (i + 1) * high, q * cols : (q + 1) * cols] = ho_ref[
+            a_ref[block + i * high : block + (i + 1) * high, q * cols : (q + 1) * cols] = ref[
                 rows + q * high : rows + (q + 1) * high, :
             ]
 
 
-def deal(info, count, heads, weights, x):
+def deal(info, count, other, mine, weights, x):
     rows, cols = x.shape
     block = rows // count
-    size = heads[0].shape[0] - rows
-    part = jax.ShapeDtypeStruct((block, cols), BF16)
+    size = mine[0].shape[0] - 2 * block
     wide = jax.ShapeDtypeStruct((block, cols), F32)
-    more = jax.ShapeDtypeStruct((block + 2 * size * heads[0].shape[1] // cols, cols), BF16)
+    more = jax.ShapeDtypeStruct((block + 2 * size * mine[0].shape[1] // cols, cols), BF16)
     return pl.pallas_call(
         functools.partial(deal_kernel, count),
-        out_shape=(wide, more, wide, part),
-        in_specs=[SMEM] + [VMEM] * 5,
-        out_specs=(VMEM,) * 4,
-        scratch_shapes=[pltpu.VMEM((rows, cols), F32)],
-        cost_estimate=pl.CostEstimate(
-            flops=4 * rows * heads[0].shape[1] * cols, bytes_accessed=4 << 20, transcendentals=0
+        out_shape=(wide, more, wide),
+        in_specs=[SMEM] + [VMEM] * 7,
+        out_specs=(VMEM,) * 3,
+        cost_estimate=pl.CostEstimate(
+            flops=3 * rows * mine[0].shape[1] * cols, bytes_accessed=4 << 20, transcendentals=0
         ),
         compiler_params=limit(12),
         name="deal",
-    )(info, *heads, *weights, x)
+    )(info, *other, *mine, *weights, x)
 
 
 def combine_kernel(mine_ref, got_ref, out_ref):
@@ -574,14 +590,13 @@
     )
     got = along(given, 1)
     own, columns = own_product(info, count, scaled, [mine, partner])
-    heads, own_state = attend(
-        info, count, width, own, given, got, resident, head_gain
-    )
-    heads_b = along(heads, 1)
-    pair = ([heads, heads_b], [out_own, outs_b])
-    given_out = outgoing(info, count, *pair, mine=False)
+    other, mine, own_state = attend(info, count, width, own, given, got, resident, head_gain)
+    other_b = along(other, 1)
+    mine_b = along(mine, 1)
+    out_pair = [out_own, outs_b]
+    given_out = outgoing([other, other_b], out_pair, BF16)
     got_out = along(given_out, 0)
-    own_out = outgoing(info, count, *pair, mine=True)
+    own_out = outgoing([mine, mine_b], out_pair, F32)
     next_mine, next_other = quarter(info, count, own_out, got_out, rows, fresh_own, fresh_partner)
     from_b = to_next(next_other, 0, 1)
     from_a = to_next(next_mine, 1, 0)
@@ -592,16 +607,20 @@
     )
     got = along(given, 1)
     (own,) = own_product(info, count, scaled, [columns])
-    heads, own_state = attend(info, count, width, own, given, got, own_state, head_gain, resident)
-    heads_b = along(heads, 1)
-    keep, to_a, to_b, cross = deal(
-        info, count, [heads, heads_b], [out_own, outs_b], rows
-    )
+    other, mine, own_state = attend(
+        info, count, width, own, given, got, own_state, head_gain, resident
+    )
+    other_b = along(other, 1)
+    mine_b = along(mine, 1)
+    cross = crossing(info, count, [other, other_b], out_pair)
     cross = along(cross, 0)
+    keep, to_a, to_b = deal(
+        info, count, [other, other_b], [mine, mine_b], out_pair, rows
+    )
     from_a = along(to_a, 0)
     to_b = combine(to_b, cross)
     from_b = along(to_b, 1)
-    second_out, final_state = last(info, count, keep, from_a, from_b, heads_b, resident, own_state)
+    second_out, final_state = last(info, count, keep, from_a, from_b, mine_b, resident, own_state)
     return (second_out[None], final_state[None])
 
 

time: 121 us -> 117 us (0.967)
  waiting for transfers between devices: 82.1 us -> 75.3 us
  starting transfers between devices: 23.8 us -> 26.5 us
    ppermute x16 -> x18, waiting for transfers between devices: 70.4 us -> 63.3 us  [along(): return lax.ppermute(value, ('section', 'row'), pairs)]
    ppermute x16 -> x18, starting transfers between devices: 19.9 us -> 22.6 us  [along(): return lax.ppermute(value, ('section', 'row'), pairs)]
  transfers between devices with their start and end apart: 19 -> 21, of which waited for: 17 -> 19; matrix products, arithmetic and copies ran while one was open for 0% -> 0% of each run, Pallas kernels for 5% -> 6%
where the time goes in v2:
time: 117 us; the launch traced here: 116 us
  waiting for transfers between devices  75.3 us (64%)
  starting transfers between devices  26.5 us (23%)
  Pallas kernels  11.8 us (10%)
  local copies, waits for them, and re-layouts  1.92 us (2%)
    ppermute x18, waiting for transfers between devices, along(): return lax.ppermute(value, ('section', 'row'), pairs)  63.3 us
    ppermute x18, starting transfers between devices, along(): return lax.ppermute(value, ('section', 'row'), pairs)  22.6 us
    ppermute x3, waiting for transfers between devices, to_next(): return lax.ppermute(value, ('section', 'row'), pairs)  12 us
    ppermute x3, starting transfers between devices, to_next(): return lax.ppermute(value, ('section', 'row'), pairs)  3.84 us
    pallas_call x2, Pallas kernels, attend(): pl.pallas_call(functools.partial(attend_kernel, count, first, width), out...  3.23 us
    pallas_call x2, Pallas kernels, given_product(): pl.pallas_call(functools.partial(given_kernel, count, first), out_shape=o...  2.75 us
  transfers between devices with their start and end apart: 21, of which 19 were waited for; matrix products, arithmetic and copies ran while one was open for 0% of the time, Pallas kernels for 6%

profile of v2, /device:TPU:0, one launch (start us, length us, event | category | flops | bytes accessed | tf_op | source)
XLA Modules:
  0.0 116.4 jit_solution(2571294187715064266)
XLA Ops:
  0.7 1.9 %copy-done.1 = bf16[1,512,3072]{2,1,0:T(8,128)(2,1)S(1)} copy-done((bf16[1,512,3072]{2,1,0:T(8,128)(2,1)S(1)}, bf16[1,512,3072]{2,1,0:T(8,128)(2,1)}, u32[]{:S(2)}) %copy-start.1) | copy-done | bytes 3145752
  3.0 3.0 %collective-permute-start.3 = (bf16[512,768]{1,0:T(8,128)(2,1)S(1)}, bf16[512,768]{1,0:T(8,128)(2,1)S(1)}, u32[]{:S(2)}, u32[]{:S(2)}) collective-permute-start(bf16[512,768]{1,0:T(8,128)(2,1)S(1)} %get-tuple-element.37), channel_id=1, source_target_pairs={{0,1},{1,0},{2,3},{3,2},{4,6},{5,7},{6,4},{7,5},{8,9},{9,8},{10,11... | collective-permute-start | bytes 2359304 | tf_op jit(solution)/shard_map/ppermute | solution.py:90
  6.1 1.6 %collective-permute-start.1 = (bf16[128,1024]{1,0:T(8,128)(2,1)S(1)}, bf16[128,1024]{1,0:T(8,128)(2,1)S(1)}, u32[]{:S(2)}, u32[]{:S(2)}) collective-permute-start(bf16[128,1024]{1,0:T(8,128)(2,1)S(1)} %get-tuple-element.35), channel_id=1, source_target_pairs={{0,2},{1,3},{2,0},{3,1},{4,5},{5,4},{6,7},{7,6},{8,10},{9,11},{10,... | collective-permute-start | bytes 786440 | tf_op jit(solution)/shard_map/ppermute | solution.py:90
  8.2 7.1 %collective-permute-done.1.refs_2_ = bf16[128,1024]{1,0:T(8,128)(2,1)S(1)} collective-permute-done((bf16[128,1024]{1,0:T(8,128)(2,1)S(1)}, bf16[128,1024]{1,0:T(8,128)(2,1)S(1)}, u32[]{:S(2)}, u32[]{:S(2)}) %collective-permute-start.1) | collective-permute-done | bytes 262176 | tf_op jit(solution)/shard_map/ppermute | solution.py:90
  15.9 1.5 %collective-permute-start.4 = (bf16[512,768]{1,0:T(8,128)(2,1)S(1)}, bf16[512,768]{1,0:T(8,128)(2,1)S(1)}, u32[]{:S(2)}, u32[]{:S(2)}) collective-permute-start(bf16[512,768]{1,0:T(8,128)(2,1)S(1)} %get-tuple-element.40), channel_id=1, source_target_pairs={{0,1},{1,0},{2,3},{3,2},{4,6},{5,7},{6,4},{7,5},{8,9},{9,8},{10,11... | collective-permute-start | bytes 2359304 | tf_op jit(solution)/shard_map/ppermute | solution.py:90
  17.3 4.2 %collective-permute-done.refs_1_ = bf16[128,1024]{1,0:T(8,128)(2,1)S(1)} collective-permute-done((bf16[128,1024]{1,0:T(8,128)(2,1)S(1)}, bf16[128,1024]{1,0:T(8,128)(2,1)S(1)}, u32[]{:S(2)}, u32[]{:S(2)}) %collective-permute-start) | collective-permute-done | bytes 262176 | tf_op jit(solution)/shard_map/ppermute | solution.py:90
  21.6 2.8 %collective-permute-done.2.refs_3_ = bf16[128,1024]{1,0:T(8,128)(2,1)S(1)} collective-permute-done((bf16[128,1024]{1,0:T(8,128)(2,1)S(1)}, bf16[128,1024]{1,0:T(8,128)(2,1)S(1)}, u32[]{:S(2)}, u32[]{:S(2)}) %collective-permute-start.2) | collective-permute-done | bytes 262176 | tf_op jit(solution)/shard_map/ppermute | solution.py:90
  25.8 1.7 %collective-permute-start.5 = (bf16[528,768]{1,0:T(8,128)(2,1)S(1)}, bf16[528,768]{1,0:T(8,128)(2,1)S(1)}, u32[]{:S(2)}, u32[]{:S(2)}) collective-permute-start(bf16[528,768]{1,0:T(8,128)(2,1)S(1)} %get-tuple-element.42.refs_1_), channel_id=1, source_target_pairs={{0,2},{1,3},{2,0},{3,1},{4,5},{5,4},{6,7},{7,6},{8,10},{9,11},{10,... | collective-permute-start | bytes 2433032 | tf_op jit(solution)/shard_map/ppermute | solution.py:90
  28.1 9.8 %collective-permute-done.4.refs_1_ = bf16[512,768]{1,0:T(8,128)(2,1)S(1)} collective-permute-done((bf16[512,768]{1,0:T(8,128)(2,1)S(1)}, bf16[512,768]{1,0:T(8,128)(2,1)S(1)}, u32[]{:S(2)}, u32[]{:S(2)}) %collective-permute-start.4) | collective-permute-done | bytes 786464 | tf_op jit(solution)/shard_map/ppermute | solution.py:90
  39.0 1.7 %collective-permute-done.5.refs_2_ = bf16[528,768]{1,0:T(8,128)(2,1)S(1)} collective-permute-done((bf16[528,768]{1,0:T(8,128)(2,1)S(1)}, bf16[528,768]{1,0:T(8,128)(2,1)S(1)}, u32[]{:S(2)}, u32[]{:S(2)}) %collective-permute-start.5) | collective-permute-done | bytes 811040 | tf_op jit(solution)/shard_map/ppermute | solution.py:90
  40.7 1.6 %attend_first.1 = (bf16[256,256]{1,0:T(8,128)(2,1)S(1)}, bf16[256,256]{1,0:T(8,128)(2,1)S(1)}, f32[2,128,128]{2,1,0:T(8,128)S(1)}) custom-call(s32[1]{0:T(128)} %bitcast.info_ref, f32[512,768]{1,0:T(8,128)S(1)} %get-tuple-element.41.refs_0_, bf16[528,768]{1,0:T(8,128)(2,1)S(1)} %get-tuple-element.42.refs_1_, ...), custom_call_target="tpu_custom_call" | custom-call | flops 167772160 | bytes 8388608 | tf_op jit(solution)/shard_map/attend_first/pallas_call | solution.py:343
  42.3 1.8 %collective-permute-start.8 = (bf16[256,256]{1,0:T(8,128)(2,1)S(1)}, bf16[256,256]{1,0:T(8,128)(2,1)S(1)}, u32[]{:S(2)}, u32[]{:S(2)}) collective-permute-start(bf16[256,256]{1,0:T(8,128)(2,1)S(1)} %get-tuple-element.46.refs_0_), channel_id=1, source_target_pairs={{0,2},{1,3},{2,0},{3,1},{4,5},{5,4},{6,7},{7,6},{8,10},{9,11},{10,... | collective-permute-start | bytes 393224 | tf_op jit(solution)/shard_map/ppermute | solution.py:90
  44.1 2.2 %collective-permute-done.7.refs_3_.refs_5_ = bf16[256,1024]{1,0:T(8,128)(2,1)S(1)} collective-permute-done((bf16[256,1024]{1,0:T(8,128)(2,1)S(1)}, bf16[256,1024]{1,0:T(8,128)(2,1)S(1)}, u32[]{:S(2)}, u32[]{:S(2)}) %collective-permute-start.7) | collective-permute-done | bytes 524320 | tf_op jit(solution)/shard_map/ppermute | solution.py:90
  46.3 1.4 %collective-permute-done.8.refs_1_ = bf16[256,256]{1,0:T(8,128)(2,1)S(1)} collective-permute-done((bf16[256,256]{1,0:T(8,128)(2,1)S(1)}, bf16[256,256]{1,0:T(8,128)(2,1)S(1)}, u32[]{:S(2)}, u32[]{:S(2)}) %collective-permute-start.8) | collective-permute-done | bytes 131104 | tf_op jit(solution)/shard_map/ppermute | solution.py:90
  48.1 1.8 %collective-permute-start.9 = (bf16[256,1024]{1,0:T(8,128)(2,1)S(1)}, bf16[256,1024]{1,0:T(8,128)(2,1)S(1)}, u32[]{:S(2)}, u32[]{:S(2)}) collective-permute-start(bf16[256,1024]{1,0:T(8,128)(2,1)S(1)} %outgoing.3), channel_id=1, source_target_pairs={{0,1},{1,0},{2,3},{3,2},{4,6},{5,7},{6,4},{7,5},{8,9},{9,8},{10,11... | collective-permute-start | bytes 1572872 | tf_op jit(solution)/shard_map/ppermute | solution.py:90
  50.6 1.6 %collective-permute-start.6 = (bf16[256,256]{1,0:T(8,128)(2,1)S(1)}, bf16[256,256]{1,0:T(8,128)(2,1)S(1)}, u32[]{:S(2)}, u32[]{:S(2)}) collective-permute-start(bf16[256,256]{1,0:T(8,128)(2,1)S(1)} %get-tuple-element.43.refs_0_), channel_id=1, source_target_pairs={{0,2},{1,3},{2,0},{3,1},{4,5},{5,4},{6,7},{7,6},{8,10},{9,11},{10,... | collective-permute-start | bytes 393224 | tf_op jit(solution)/shard_map/ppermute | solution.py:90
  52.2 4.8 %collective-permute-done.6.refs_1_ = bf16[256,256]{1,0:T(8,128)(2,1)S(1)} collective-permute-done((bf16[256,256]{1,0:T(8,128)(2,1)S(1)}, bf16[256,256]{1,0:T(8,128)(2,1)S(1)}, u32[]{:S(2)}, u32[]{:S(2)}) %collective-permute-start.6) | collective-permute-done | bytes 131104 | tf_op jit(solution)/shard_map/ppermute | solution.py:90
  59.0 1.5 %collective-permute-start.13 = (bf16[256,512]{1,0:T(8,128)(2,1)S(1)}, bf16[256,512]{1,0:T(8,128)(2,1)S(1)}, u32[]{:S(2)}, u32[]{:S(2)}) collective-permute-start(bf16[256,512]{1,0:T(8,128)(2,1)S(1)} %get-tuple-element.51), channel_id=1, source_target_pairs={{0,5},{1,4},{2,7},{3,6},{4,10},{5,11},{6,8},{7,9},{8,13},{9,12},{1... | collective-permute-start | bytes 786440 | tf_op jit(solution)/shard_map/ppermute | solution.py:100
  60.5 1.4 %collective-permute-start.11 = (bf16[256,512]{1,0:T(8,128)(2,1)S(1)}, bf16[256,512]{1,0:T(8,128)(2,1)S(1)}, u32[]{:S(2)}, u32[]{:S(2)}) collective-permute-start(bf16[256,512]{1,0:T(8,128)(2,1)S(1)} %get-tuple-element.50), channel_id=1, source_target_pairs={{0,4},{1,5},{2,6},{3,7},{4,8},{5,9},{6,10},{7,11},{8,12},{9,13},{1... | collective-permute-start | bytes 786440 | tf_op jit(solution)/shard_map/ppermute | solution.py:100
  62.9 7.9 %collective-permute-done.13.refs_2_ = bf16[256,512]{1,0:T(8,128)(2,1)S(1)} collective-permute-done((bf16[256,512]{1,0:T(8,128)(2,1)S(1)}, bf16[256,512]{1,0:T(8,128)(2,1)S(1)}, u32[]{:S(2)}, u32[]{:S(2)}) %collective-permute-start.13) | collective-permute-done | bytes 262176 | tf_op jit(solution)/shard_map/ppermute | solution.py:100
  70.8 1.5 %collective-permute-start.14 = (bf16[256,512]{1,0:T(8,128)(2,1)S(1)}, bf16[256,512]{1,0:T(8,128)(2,1)S(1)}, u32[]{:S(2)}, u32[]{:S(2)}) collective-permute-start(bf16[256,512]{1,0:T(8,128)(2,1)S(1)} %collective-permute-done.13.refs_2_), channel_id=1, source_target_pairs={{0,1},{1,0},{2,3},{3,2},{4,6},{5,7},{6,4},{7,5},{8,9},{9,8},{10,11... | collective-permute-start | bytes 786440 | tf_op jit(solution)/shard_map/ppermute | solution.py:90
  72.6 3.8 %collective-permute-done.12.refs_1_ = bf16[256,512]{1,0:T(8,128)(2,1)S(1)} collective-permute-done((bf16[256,512]{1,0:T(8,128)(2,1)S(1)}, bf16[256,512]{1,0:T(8,128)(2,1)S(1)}, u32[]{:S(2)}, u32[]{:S(2)}) %collective-permute-start.12) | collective-permute-done | bytes 262176 | tf_op jit(solution)/shard_map/ppermute | solution.py:100
  76.4 3.9 %collective-permute-done.14.refs_3_ = bf16[256,512]{1,0:T(8,128)(2,1)S(1)} collective-permute-done((bf16[256,512]{1,0:T(8,128)(2,1)S(1)}, bf16[256,512]{1,0:T(8,128)(2,1)S(1)}, u32[]{:S(2)}, u32[]{:S(2)}) %collective-permute-start.14) | collective-permute-done | bytes 262176 | tf_op jit(solution)/shard_map/ppermute | solution.py:90
  81.7 1.7 %collective-permute-start.15 = (bf16[528,768]{1,0:T(8,128)(2,1)S(1)}, bf16[528,768]{1,0:T(8,128)(2,1)S(1)}, u32[]{:S(2)}, u32[]{:S(2)}) collective-permute-start(bf16[528,768]{1,0:T(8,128)(2,1)S(1)} %get-tuple-element.55.refs_1_), channel_id=1, source_target_pairs={{0,2},{1,3},{2,0},{3,1},{4,5},{5,4},{6,7},{7,6},{8,10},{9,11},{10,... | collective-permute-start | bytes 2433032 | tf_op jit(solution)/shard_map/ppermute | solution.py:90
  84.3 9.7 %collective-permute-done.15.refs_2_ = bf16[528,768]{1,0:T(8,128)(2,1)S(1)} collective-permute-done((bf16[528,768]{1,0:T(8,128)(2,1)S(1)}, bf16[528,768]{1,0:T(8,128)(2,1)S(1)}, u32[]{:S(2)}, u32[]{:S(2)}) %collective-permute-start.15) | collective-permute-done | bytes 811040 | tf_op jit(solution)/shard_map/ppermute | solution.py:90
  94.0 1.6 %attend_second.1 = (bf16[256,256]{1,0:T(8,128)(2,1)S(1)}, bf16[384,256]{1,0:T(8,128)(2,1)S(1)}, f32[2,128,128]{2,1,0:T(8,128)S(1)}) custom-call(s32[1]{0:T(128)} %bitcast.info_ref, f32[512,768]{1,0:T(8,128)S(1)} %own_second.1.refs_0_, bf16[528,768]{1,0:T(8,128)(2,1)S(1)} %get-tuple-element.55.refs_1_, bf16[528,768]{1,0:T(8,128)(2,1)S(1)} %collective-permute-done.15.refs_2_, ...), custom_call_target="tpu_custom_call" | custom-call | flops 167772160 | bytes 8388608 | tf_op jit(solution)/shard_map/attend_second/pallas_call | solution.py:343
  95.6 1.7 %collective-permute-start.16 = (bf16[256,256]{1,0:T(8,128)(2,1)S(1)}, bf16[256,256]{1,0:T(8,128)(2,1)S(1)}, u32[]{:S(2)}, u32[]{:S(2)}) collective-permute-start(bf16[256,256]{1,0:T(8,128)(2,1)S(1)} %get-tuple-element.57.refs_0_), channel_id=1, source_target_pairs={{0,2},{1,3},{2,0},{3,1},{4,5},{5,4},{6,7},{7,6},{8,10},{9,11},{10,... | collective-permute-start | bytes 393224 | tf_op jit(solution)/shard_map/ppermute | solution.py:90
  97.7 4.3 %collective-permute-done.16.refs_1_ = bf16[256,256]{1,0:T(8,128)(2,1)S(1)} collective-permute-done((bf16[256,256]{1,0:T(8,128)(2,1)S(1)}, bf16[256,256]{1,0:T(8,128)(2,1)S(1)}, u32[]{:S(2)}, u32[]{:S(2)}) %collective-permute-start.16) | collective-permute-done | bytes 131104 | tf_op jit(solution)/shard_map/ppermute | solution.py:90
  102.6 3.6 %collective-permute-done.17.refs_3_.heads_ref = bf16[384,256]{1,0:T(8,128)(2,1)S(1)} collective-permute-done((bf16[384,256]{1,0:T(8,128)(2,1)S(1)}, bf16[384,256]{1,0:T(8,128)(2,1)S(1)}, u32[]{:S(2)}, u32[]{:S(2)}) %collective-permute-start.17) | collective-permute-done | bytes 196640 | tf_op jit(solution)/shard_map/ppermute | solution.py:90
  107.1 1.7 %collective-permute-done.19.got_ref = bf16[128,1024]{1,0:T(8,128)(2,1)S(1)} collective-permute-done((bf16[128,1024]{1,0:T(8,128)(2,1)S(1)}, bf16[128,1024]{1,0:T(8,128)(2,1)S(1)}, u32[]{:S(2)}, u32[]{:S(2)}) %collective-permute-start.19) | collective-permute-done | bytes 262176 | tf_op jit(solution)/shard_map/ppermute | solution.py:90
  108.8 1.7 %collective-permute-start.20 = (bf16[128,1024]{1,0:T(8,128)(2,1)S(1)}, bf16[128,1024]{1,0:T(8,128)(2,1)S(1)}, u32[]{:S(2)}, u32[]{:S(2)}) collective-permute-start(bf16[128,1024]{1,0:T(8,128)(2,1)S(1)} %combine.1), channel_id=1, source_target_pairs={{0,2},{1,3},{2,0},{3,1},{4,5},{5,4},{6,7},{7,6},{8,10},{9,11},{10,... | collective-permute-start | bytes 786440 | tf_op jit(solution)/shard_map/ppermute | solution.py:90
  110.5 4.2 %collective-permute-done.18.a_ref = bf16[192,1024]{1,0:T(8,128)(2,1)S(1)} collective-permute-done((bf16[192,1024]{1,0:T(8,128)(2,1)S(1)}, bf16[192,1024]{1,0:T(8,128)(2,1)S(1)}, u32[]{:S(2)}, u32[]{:S(2)}) %collective-permute-start.18) | collective-permute-done | bytes 393248 | tf_op jit(solution)/shard_map/ppermute | solution.py:90
  (40 shorter events, 15.0 us)
Async XLA Ops:
  0.7 1.9 %copy-start.1 = (bf16[1,512,3072]{2,1,0:T(8,128)(2,1)S(1)}, bf16[1,512,3072]{2,1,0:T(8,128)(2,1)}, u32[]{:S(2)}) copy-start(bf16[1,512,3072]{2,1,0:T(8,128)(2,1)} %param.10) | copy-start | bytes 9437188
  2.5 3.4 %copy-start.3 = (bf16[1,128,2048]{2,1,0:T(8,128)(2,1)S(1)}, bf16[1,128,2048]{2,1,0:T(8,128)(2,1)}, u32[]{:S(2)}) copy-start(bf16[1,128,2048]{2,1,0:T(8,128)(2,1)} %param.7) | copy-start | bytes 1572868
  2.5 21.8 %copy-start.6 = (f32[1,2048]{1,0:T(1,128)S(1)}, f32[1,2048]{1,0:T(1,128)}, u32[]{:S(2)}) copy-start(f32[1,2048]{1,0:T(1,128)} %gain_ref.3) | copy-start | bytes 24580
  3.0 21.4 %collective-permute-start.3 = (bf16[512,768]{1,0:T(8,128)(2,1)S(1)}, bf16[512,768]{1,0:T(8,128)(2,1)S(1)}, u32[]{:S(2)}, u32[]{:S(2)}) collective-permute-start(bf16[512,768]{1,0:T(8,128)(2,1)S(1)} %get-tuple-element.37), channel_id=1, source_target_pairs={{0,1},{1,0},{2,3},{3,2},{4,6},{5,7},{6,4},{7,5},{8,9},{9,8},{10,11... | collective-permute-start | bytes 2359304 | tf_op jit(solution)/shard_map/ppermute | solution.py:90
  6.0 21.4 %copy-start.2 = (bf16[1,256,2048]{2,1,0:T(8,128)(2,1)S(1)}, bf16[1,256,2048]{2,1,0:T(8,128)(2,1)}, u32[]{:S(2)}) copy-start(bf16[1,256,2048]{2,1,0:T(8,128)(2,1)} %param.11) | copy-start | bytes 3145732
  6.0 21.4 %copy-start.4 = (bf16[128,2048]{1,0:T(8,128)(2,1)S(1)}, bf16[128,2048]{1,0:T(8,128)(2,1)}, u32[]{:S(2)}) copy-start(bf16[128,2048]{1,0:T(8,128)(2,1)} %refs_1_.1) | copy-start | bytes 1572868
  6.1 9.2 %collective-permute-start.1 = (bf16[128,1024]{1,0:T(8,128)(2,1)S(1)}, bf16[128,1024]{1,0:T(8,128)(2,1)S(1)}, u32[]{:S(2)}, u32[]{:S(2)}) collective-permute-start(bf16[128,1024]{1,0:T(8,128)(2,1)S(1)} %get-tuple-element.35), channel_id=1, source_target_pairs={{0,2},{1,3},{2,0},{3,1},{4,5},{5,4},{6,7},{7,6},{8,10},{9,11},{10,... | collective-permute-start | bytes 786440 | tf_op jit(solution)/shard_map/ppermute | solution.py:90
  7.6 13.9 %collective-permute-start = (bf16[128,1024]{1,0:T(8,128)(2,1)S(1)}, bf16[128,1024]{1,0:T(8,128)(2,1)S(1)}, u32[]{:S(2)}, u32[]{:S(2)}) collective-permute-start(bf16[128,1024]{1,0:T(8,128)(2,1)S(1)} %get-tuple-element.34.refs_0_), channel_id=1, source_target_pairs={{0,1},{1,0},{2,3},{3,2},{4,6},{5,7},{6,4},{7,5},{8,9},{9,8},{10,11... | collective-permute-start | bytes 786440 | tf_op jit(solution)/shard_map/ppermute | solution.py:90
  15.3 9.1 %collective-permute-start.2 = (bf16[128,1024]{1,0:T(8,128)(2,1)S(1)}, bf16[128,1024]{1,0:T(8,128)(2,1)S(1)}, u32[]{:S(2)}, u32[]{:S(2)}) collective-permute-start(bf16[128,1024]{1,0:T(8,128)(2,1)S(1)} %collective-permute-done.1.refs_2_), channel_id=1, source_target_pairs={{0,1},{1,0},{2,3},{3,2},{4,6},{5,7},{6,4},{7,5},{8,9},{9,8},{10,11... | collective-permute-start | bytes 786440 | tf_op jit(solution)/shard_map/ppermute | solution.py:90
  15.9 22.0 %collective-permute-start.4 = (bf16[512,768]{1,0:T(8,128)(2,1)S(1)}, bf16[512,768]{1,0:T(8,128)(2,1)S(1)}, u32[]{:S(2)}, u32[]{:S(2)}) collective-permute-start(bf16[512,768]{1,0:T(8,128)(2,1)S(1)} %get-tuple-element.40), channel_id=1, source_target_pairs={{0,1},{1,0},{2,3},{3,2},{4,6},{5,7},{6,4},{7,5},{8,9},{9,8},{10,11... | collective-permute-start | bytes 2359304 | tf_op jit(solution)/shard_map/ppermute | solution.py:90
  25.8 14.9 %collective-permute-start.5 = (bf16[528,768]{1,0:T(8,128)(2,1)S(1)}, bf16[528,768]{1,0:T(8,128)(2,1)S(1)}, u32[]{:S(2)}, u32[]{:S(2)}) collective-permute-start(bf16[528,768]{1,0:T(8,128)(2,1)S(1)} %get-tuple-element.42.refs_1_), channel_id=1, source_target_pairs={{0,2},{1,3},{2,0},{3,1},{4,5},{5,4},{6,7},{7,6},{8,10},{9,11},{10,... | collective-permute-start | bytes 2433032 | tf_op jit(solution)/shard_map/ppermute | solution.py:90
  27.6 13.1 %copy-start = (f32[1,8,128,128]{3,2,1,0:T(8,128)S(1)}, f32[1,8,128,128]{3,2,1,0:T(8,128)}, u32[]{:S(2)}) copy-start(f32[1,8,128,128]{3,2,1,0:T(8,128)} %param.9) | copy-start | bytes 1572868
  27.6 13.1 %copy-start.5 = (f32[1,1024]{1,0:T(1,128)S(1)}, f32[1,1024]{1,0:T(1,128)}, u32[]{:S(2)}) copy-start(f32[1,1024]{1,0:T(1,128)} %refs_4_.3) | copy-start | bytes 12292
  27.6 18.7 %collective-permute-start.7 = (bf16[256,1024]{1,0:T(8,128)(2,1)S(1)}, bf16[256,1024]{1,0:T(8,128)(2,1)S(1)}, u32[]{:S(2)}, u32[]{:S(2)}) collective-permute-start(bf16[256,1024]{1,0:T(8,128)(2,1)S(1)} %get-tuple-element.45), channel_id=1, source_target_pairs={{0,2},{1,3},{2,0},{3,1},{4,5},{5,4},{6,7},{7,6},{8,10},{9,11},{10,... | collective-permute-start | bytes 1572872 | tf_op jit(solution)/shard_map/ppermute | solution.py:90
  42.3 5.4 %collective-permute-start.8 = (bf16[256,256]{1,0:T(8,128)(2,1)S(1)}, bf16[256,256]{1,0:T(8,128)(2,1)S(1)}, u32[]{:S(2)}, u32[]{:S(2)}) collective-permute-start(bf16[256,256]{1,0:T(8,128)(2,1)S(1)} %get-tuple-element.46.refs_0_), channel_id=1, source_target_pairs={{0,2},{1,3},{2,0},{3,1},{4,5},{5,4},{6,7},{7,6},{8,10},{9,11},{10,... | collective-permute-start | bytes 393224 | tf_op jit(solution)/shard_map/ppermute | solution.py:90
  48.1 10.7 %collective-permute-start.9 = (bf16[256,1024]{1,0:T(8,128)(2,1)S(1)}, bf16[256,1024]{1,0:T(8,128)(2,1)S(1)}, u32[]{:S(2)}, u32[]{:S(2)}) collective-permute-start(bf16[256,1024]{1,0:T(8,128)(2,1)S(1)} %outgoing.3), channel_id=1, source_target_pairs={{0,1},{1,0},{2,3},{3,2},{4,6},{5,7},{6,4},{7,5},{8,9},{9,8},{10,11... | collective-permute-start | bytes 1572872 | tf_op jit(solution)/shard_map/ppermute | solution.py:90
  49.9 7.6 %collective-permute-start.10 = (bf16[128,1024]{1,0:T(8,128)(2,1)S(1)}, bf16[128,1024]{1,0:T(8,128)(2,1)S(1)}, u32[]{:S(2)}, u32[]{:S(2)}) collective-permute-start(bf16[128,1024]{1,0:T(8,128)(2,1)S(1)} %get-tuple-element.49), channel_id=1, source_target_pairs={{28,29},{29,28},{30,31},{31,30}} | collective-permute-start | bytes 786440 | tf_op jit(solution)/shard_map/ppermute | solution.py:90
  50.6 6.4 %collective-permute-start.6 = (bf16[256,256]{1,0:T(8,128)(2,1)S(1)}, bf16[256,256]{1,0:T(8,128)(2,1)S(1)}, u32[]{:S(2)}, u32[]{:S(2)}) collective-permute-start(bf16[256,256]{1,0:T(8,128)(2,1)S(1)} %get-tuple-element.43.refs_0_), channel_id=1, source_target_pairs={{0,2},{1,3},{2,0},{3,1},{4,5},{5,4},{6,7},{7,6},{8,10},{9,11},{10,... | collective-permute-start | bytes 393224 | tf_op jit(solution)/shard_map/ppermute | solution.py:90
  59.0 11.7 %collective-permute-start.13 = (bf16[256,512]{1,0:T(8,128)(2,1)S(1)}, bf16[256,512]{1,0:T(8,128)(2,1)S(1)}, u32[]{:S(2)}, u32[]{:S(2)}) collective-permute-start(bf16[256,512]{1,0:T(8,128)(2,1)S(1)} %get-tuple-element.51), channel_id=1, source_target_pairs={{0,5},{1,4},{2,7},{3,6},{4,10},{5,11},{6,8},{7,9},{8,13},{9,12},{1... | collective-permute-start | bytes 786440 | tf_op jit(solution)/shard_map/ppermute | solution.py:100
  60.5 12.1 %collective-permute-start.11 = (bf16[256,512]{1,0:T(8,128)(2,1)S(1)}, bf16[256,512]{1,0:T(8,128)(2,1)S(1)}, u32[]{:S(2)}, u32[]{:S(2)}) collective-permute-start(bf16[256,512]{1,0:T(8,128)(2,1)S(1)} %get-tuple-element.50), channel_id=1, source_target_pairs={{0,4},{1,5},{2,6},{3,7},{4,8},{5,9},{6,10},{7,11},{8,12},{9,13},{1... | collective-permute-start | bytes 786440 | tf_op jit(solution)/shard_map/ppermute | solution.py:100
  62.0 14.4 %collective-permute-start.12 = (bf16[256,512]{1,0:T(8,128)(2,1)S(1)}, bf16[256,512]{1,0:T(8,128)(2,1)S(1)}, u32[]{:S(2)}, u32[]{:S(2)}) collective-permute-start(bf16[256,512]{1,0:T(8,128)(2,1)S(1)} %get-tuple-element.50), channel_id=1, source_target_pairs={{0,6},{1,7},{2,4},{3,5},{4,9},{5,8},{6,11},{7,10},{8,14},{9,15},{1... | collective-permute-start | bytes 786440 | tf_op jit(solution)/shard_map/ppermute | solution.py:100
  70.8 9.5 %collective-permute-start.14 = (bf16[256,512]{1,0:T(8,128)(2,1)S(1)}, bf16[256,512]{1,0:T(8,128)(2,1)S(1)}, u32[]{:S(2)}, u32[]{:S(2)}) collective-permute-start(bf16[256,512]{1,0:T(8,128)(2,1)S(1)} %collective-permute-done.13.refs_2_), channel_id=1, source_target_pairs={{0,1},{1,0},{2,3},{3,2},{4,6},{5,7},{6,4},{7,5},{8,9},{9,8},{10,11... | collective-permute-start | bytes 786440 | tf_op jit(solution)/shard_map/ppermute | solution.py:90
  81.7 12.3 %collective-permute-start.15 = (bf16[528,768]{1,0:T(8,128)(2,1)S(1)}, bf16[528,768]{1,0:T(8,128)(2,1)S(1)}, u32[]{:S(2)}, u32[]{:S(2)}) collective-permute-start(bf16[528,768]{1,0:T(8,128)(2,1)S(1)} %get-tuple-element.55.refs_1_), channel_id=1, source_target_pairs={{0,2},{1,3},{2,0},{3,1},{4,5},{5,4},{6,7},{7,6},{8,10},{9,11},{10,... | collective-permute-start | bytes 2433032 | tf_op jit(solution)/shard_map/ppermute | solution.py:90
  95.6 6.4 %collective-permute-start.16 = (bf16[256,256]{1,0:T(8,128)(2,1)S(1)}, bf16[256,256]{1,0:T(8,128)(2,1)S(1)}, u32[]{:S(2)}, u32[]{:S(2)}) collective-permute-start(bf16[256,256]{1,0:T(8,128)(2,1)S(1)} %get-tuple-element.57.refs_0_), channel_id=1, source_target_pairs={{0,2},{1,3},{2,0},{3,1},{4,5},{5,4},{6,7},{7,6},{8,10},{9,11},{10,... | collective-permute-start | bytes 393224 | tf_op jit(solution)/shard_map/ppermute | solution.py:90
  97.3 9.0 %collective-permute-start.17 = (bf16[384,256]{1,0:T(8,128)(2,1)S(1)}, bf16[384,256]{1,0:T(8,128)(2,1)S(1)}, u32[]{:S(2)}, u32[]{:S(2)}) collective-permute-start(bf16[384,256]{1,0:T(8,128)(2,1)S(1)} %get-tuple-element.58.refs_2_), channel_id=1, source_target_pairs={{0,2},{1,3},{2,0},{3,1},{4,5},{5,4},{6,7},{7,6},{8,10},{9,11},{10,... | collective-permute-start | bytes 589832 | tf_op jit(solution)/shard_map/ppermute | solution.py:90
  102.4 6.4 %collective-permute-start.19 = (bf16[128,1024]{1,0:T(8,128)(2,1)S(1)}, bf16[128,1024]{1,0:T(8,128)(2,1)S(1)}, u32[]{:S(2)}, u32[]{:S(2)}) collective-permute-start(bf16[128,1024]{1,0:T(8,128)(2,1)S(1)} %crossing.1), channel_id=1, source_target_pairs={{0,1},{1,0},{2,3},{3,2},{4,6},{5,7},{6,4},{7,5},{8,9},{9,8},{10,11... | collective-permute-start | bytes 786440 | tf_op jit(solution)/shard_map/ppermute | solution.py:90
  106.8 7.8 %collective-permute-start.18 = (bf16[192,1024]{1,0:T(8,128)(2,1)S(1)}, bf16[192,1024]{1,0:T(8,128)(2,1)S(1)}, u32[]{:S(2)}, u32[]{:S(2)}) collective-permute-start(bf16[192,1024]{1,0:T(8,128)(2,1)S(1)} %get-tuple-element.61), channel_id=1, source_target_pairs={{0,1},{1,0},{2,3},{3,2},{4,6},{5,7},{6,4},{7,5},{8,9},{9,8},{10,11... | collective-permute-start | bytes 1179656 | tf_op jit(solution)/shard_map/ppermute | solution.py:90
  108.8 6.4 %collective-permute-start.20 = (bf16[128,1024]{1,0:T(8,128)(2,1)S(1)}, bf16[128,1024]{1,0:T(8,128)(2,1)S(1)}, u32[]{:S(2)}, u32[]{:S(2)}) collective-permute-start(bf16[128,1024]{1,0:T(8,128)(2,1)S(1)} %combine.1), channel_id=1, source_target_pairs={{0,2},{1,3},{2,0},{3,1},{4,5},{5,4},{6,7},{7,6},{8,10},{9,11},{10,... | collective-permute-start | bytes 786440 | tf_op jit(solution)/shard_map/ppermute | solution.py:90

commit v3 on v2

--- a/solution.py
+++ b/solution.py
@@ -365,64 +365,71 @@
     return total
 
 
-def outgoing_kernel(*refs):
-    out_ref = refs[4]
-    out_ref[...] = product_of(refs[:2], refs[2:4], slice(None)).astype(out_ref.dtype)
-
-
-def outgoing(heads, weights, dtype):
+def outgoing_kernel(count, parts, info_ref, *refs):
+    me, _, bit_a, _ = whereabouts(info_ref, count)
+    ho_refs, w_refs, outs = refs[:2], refs[2:4], refs[4:]
+    if parts == 1:
+        outs[0][...] = product_of(ho_refs, w_refs, slice(None)).astype(outs[0].dtype)
+        return
+    width = outs[0].shape[1]
+    second = (me & bit_a) // bit_a
+    for out_ref, part in ((outs[0], second), (outs[1], 1 - second)):
+        columns = pl.ds(pl.multiple_of(part * width, width), width)
+        total = None
+        for ho_ref, w_ref in zip(ho_refs, w_refs):
+            term = jnp.dot(ho_ref[...], w_ref[:, columns], preferred_element_type=F32)
+            total = term if total is None else total + term
+        out_ref[...] = total.astype(out_ref.dtype)
+
+
+def outgoing(info, count, heads, weights, dtype, parts):
     rows, depth = heads[0].shape
     cols = weights[0].shape[1]
     return pl.pallas_call(
-        outgoing_kernel,
-        out_shape=jax.ShapeDtypeStruct((rows, cols), dtype),
-        in_specs=[VMEM] * 4,
-        out_specs=VMEM,
+        functools.partial(outgoing_kernel, count, parts),
+        out_shape=[jax.ShapeDtypeStruct((rows, cols // parts), dtype)] * parts,
+        in_specs=[SMEM] + [VMEM] * 4,
+        out_specs=[VMEM] * parts,
         cost_estimate=pl.CostEstimate(
             flops=4 * rows * depth * cols, bytes_accessed=4 << 20, transcendentals=0
         ),
         compiler_params=limit(9),
-        name="outgoing",
-    )(*heads, *weights)
-
-
-def quarter_kernel(count, info_ref, own_ref, got_ref, x_ref, fresh_ref, partner_ref, *refs):
-    next_mine, next_other, quarter = refs
+        name="outgoing_mine" if parts == 1 else "outgoing_given",
+    )(info, *heads, *weights)
+
+
+def quarter_kernel(count, mine, info_ref, own_ref, got_ref, x_ref, fresh_ref, partner_ref, out_ref):
     me, place, bit_a, bit_b = whereabouts(info_ref, count)
-    block, depth = fresh_ref.shape[0], own_ref.shape[1] // 2
-    second = (me & bit_b) // bit_b
-    here = pl.ds(pl.multiple_of(second * block, block), block)
-    there = pl.ds(pl.multiple_of((1 - second) * block, block), block)
+    block, depth = fresh_ref.shape[0], out_ref.shape[1]
+    part = (me & bit_a) // bit_a
+    part = part if mine else 1 - part
+    columns = pl.ds(pl.multiple_of(part * depth, depth), depth)
     for t in range(2):
         rows = slice(t * block, (t + 1) * block)
         at = pl.multiple_of(((me & bit_a) | (t * bit_b)) * block, block)
-        x = x_ref[pl.ds(at, block), :].astype(F32)
-        quarter[rows, :] = (x + own_ref[rows, :] + got_ref[rows, :].astype(F32)).astype(BF16)
+        x = x_ref[pl.ds(at, block), columns].astype(F32)
+        out_ref[rows, :] = (x + own_ref[rows, columns] + got_ref[rows, :].astype(F32)).astype(BF16)
 
     @pl.when(place == 1)
     def _():
-        quarter[here, :] = fresh_ref[...]
-        quarter[there, :] = partner_ref[...]
-
-    part = (me & bit_a) // bit_a
-    next_mine[...] = quarter[:, pl.ds(pl.multiple_of(part * depth, depth), depth)]
-    next_other[...] = quarter[:, pl.ds(pl.multiple_of((1 - part) * depth, depth), depth)]
-
-
-def quarter(info, count, own, got, x, fresh, fresh_partner):
-    rows, cols = own.shape
-    block = jax.ShapeDtypeStruct((rows, cols // 2), BF16)
-    return pl.pallas_call(
-        functools.partial(quarter_kernel, count),
-        out_shape=(block, block),
+        second = (me & bit_b) // bit_b
+        here = pl.ds(pl.multiple_of(second * block, block), block)
+        there = pl.ds(pl.multiple_of((1 - second) * block, block), block)
+        out_ref[here, :] = fresh_ref[:, columns]
+        out_ref[there, :] = partner_ref[:, columns]
+
+
+def quarter(info, count, own, got, x, fresh, fresh_partner, mine):
+    return pl.pallas_call(
+        functools.partial(quarter_kernel, count, mine),
+        out_shape=jax.ShapeDtypeStruct(got.shape, BF16),
         in_specs=[SMEM] + [VMEM] * 5,
-        out_specs=(VMEM, VMEM),
-        scratch_shapes=[pltpu.VMEM((rows, cols), BF16)],
-        cost_estimate=pl.CostEstimate(
-            flops=4 * rows * cols, bytes_accessed=4 << 20, transcendentals=0
+        out_specs=VMEM,
+        cost_estimate=pl.CostEstimate(
+            flops=4 * got.size, bytes_accessed=4 << 20, transcendentals=0
         ),
         compiler_params=limit(9),
-        name="quarter",
+        name="quarter_mine" if mine else "quarter_other",
     )(info, own, got, x, fresh, fresh_partner)
 
 
@@ -594,11 +601,14 @@
     other_b = along(other, 1)
     mine_b = along(mine, 1)
     out_pair = [out_own, outs_b]
-    given_out = outgoing([other, other_b], out_pair, BF16)
+    given_out, given_late = outgoing(info, count, [other, other_b], out_pair, BF16, 2)
     got_out = along(given_out, 0)
-    own_out = outgoing([mine, mine_b], out_pair, F32)
-    next_mine, next_other = quarter(info, count, own_out, got_out, rows, fresh_own, fresh_partner)
+    got_late = along(given_late, 0)
+    (own_out,) = outgoing(info, count, [mine, mine_b], out_pair, F32, 1)
+    residual = (rows, fresh_own, fresh_partner)
+    next_other = quarter(info, count, own_out, got_out, *residual, mine=False)
     from_b = to_next(next_other, 0, 1)
+    next_mine = quarter(info, count, own_out, got_late, *residual, mine=True)
     from_a = to_next(next_mine, 1, 0)
     own_half = to_next(next_mine, 0, 0)
     from_far = along(from_b, 0)

time: 117 us -> 113 us (0.966)
  waiting for transfers between devices: 75.3 us -> 72.9 us
    ppermute x3, waiting for transfers between devices: 12 us -> 8.64 us  [to_next(): return lax.ppermute(value, ('section', 'row'), pairs)]
    ppermute x18 -> x19, waiting for transfers between devices: 63.3 us -> 64.2 us  [along(): return lax.ppermute(value, ('section', 'row'), pairs)]
    ppermute x18 -> x19, starting transfers between devices: 22.6 us -> 21.7 us  [along(): return lax.ppermute(value, ('section', 'row'), pairs)]
  transfers between devices with their start and end apart: 21 -> 22, of which waited for: 19 -> 19; matrix products, arithmetic and copies ran while one was open for 0% -> 0% of each run, Pallas kernels for 6% -> 7%
where the time goes in v3:
time: 113 us
  waiting for transfers between devices  72.9 us (65%)
  starting transfers between devices  25.5 us (23%)
  Pallas kernels  11.8 us (10%)
  local copies, waits for them, and re-layouts  1.92 us (2%)
    ppermute x19, waiting for transfers between devices, along(): return lax.ppermute(value, ('section', 'row'), pairs)  64.2 us
    ppermute x19, starting transfers between devices, along(): return lax.ppermute(value, ('section', 'row'), pairs)  21.7 us
    ppermute x3, waiting for transfers between devices, to_next(): return lax.ppermute(value, ('section', 'row'), pairs)  8.64 us
    ppermute x3, starting transfers between devices, to_next(): return lax.ppermute(value, ('section', 'row'), pairs)  3.78 us
    pallas_call x2, Pallas kernels, attend(): pl.pallas_call(functools.partial(attend_kernel, count, first, width), out...  3.23 us
    pallas_call x2, Pallas kernels, given_product(): pl.pallas_call(functools.partial(given_kernel, count, first), out_shape=o...  2.75 us
  transfers between devices with their start and end apart: 22, of which 19 were waited for; matrix products, arithmetic and copies ran while one was open for 0% of the time, Pallas kernels for 7%

profile of v3, /device:TPU:0, one launch (start us, length us, event | category | flops | bytes accessed | tf_op | source)
XLA Modules:
  0.0 112.9 jit_solution(13835646989438424057)
XLA Ops:
  0.7 1.9 %copy-done.1 = bf16[1,512,3072]{2,1,0:T(8,128)(2,1)S(1)} copy-done((bf16[1,512,3072]{2,1,0:T(8,128)(2,1)S(1)}, bf16[1,512,3072]{2,1,0:T(8,128)(2,1)}, u32[]{:S(2)}) %copy-start.1) | copy-done | bytes 3145752
  3.0 3.0 %collective-permute-start.3 = (bf16[512,768]{1,0:T(8,128)(2,1)S(1)}, bf16[512,768]{1,0:T(8,128)(2,1)S(1)}, u32[]{:S(2)}, u32[]{:S(2)}) collective-permute-start(bf16[512,768]{1,0:T(8,128)(2,1)S(1)} %get-tuple-element.37), channel_id=1, source_target_pairs={{0,1},{1,0},{2,3},{3,2},{4,6},{5,7},{6,4},{7,5},{8,9},{9,8},{10,11... | collective-permute-start | bytes 2359304 | tf_op jit(solution)/shard_map/ppermute | solution.py:90
  6.1 1.6 %collective-permute-start.1 = (bf16[128,1024]{1,0:T(8,128)(2,1)S(1)}, bf16[128,1024]{1,0:T(8,128)(2,1)S(1)}, u32[]{:S(2)}, u32[]{:S(2)}) collective-permute-start(bf16[128,1024]{1,0:T(8,128)(2,1)S(1)} %get-tuple-element.35), channel_id=1, source_target_pairs={{0,2},{1,3},{2,0},{3,1},{4,5},{5,4},{6,7},{7,6},{8,10},{9,11},{10,... | collective-permute-start | bytes 786440 | tf_op jit(solution)/shard_map/ppermute | solution.py:90
  8.2 7.1 %collective-permute-done.1.refs_2_ = bf16[128,1024]{1,0:T(8,128)(2,1)S(1)} collective-permute-done((bf16[128,1024]{1,0:T(8,128)(2,1)S(1)}, bf16[128,1024]{1,0:T(8,128)(2,1)S(1)}, u32[]{:S(2)}, u32[]{:S(2)}) %collective-permute-start.1) | collective-permute-done | bytes 262176 | tf_op jit(solution)/shard_map/ppermute | solution.py:90
  15.9 1.5 %collective-permute-start.4 = (bf16[512,768]{1,0:T(8,128)(2,1)S(1)}, bf16[512,768]{1,0:T(8,128)(2,1)S(1)}, u32[]{:S(2)}, u32[]{:S(2)}) collective-permute-start(bf16[512,768]{1,0:T(8,128)(2,1)S(1)} %get-tuple-element.40), channel_id=1, source_target_pairs={{0,1},{1,0},{2,3},{3,2},{4,6},{5,7},{6,4},{7,5},{8,9},{9,8},{10,11... | collective-permute-start | bytes 2359304 | tf_op jit(solution)/shard_map/ppermute | solution.py:90
  17.3 4.2 %collective-permute-done.refs_1_ = bf16[128,1024]{1,0:T(8,128)(2,1)S(1)} collective-permute-done((bf16[128,1024]{1,0:T(8,128)(2,1)S(1)}, bf16[128,1024]{1,0:T(8,128)(2,1)S(1)}, u32[]{:S(2)}, u32[]{:S(2)}) %collective-permute-start) | collective-permute-done | bytes 262176 | tf_op jit(solution)/shard_map/ppermute | solution.py:90
  21.6 2.8 %collective-permute-done.2.refs_3_ = bf16[128,1024]{1,0:T(8,128)(2,1)S(1)} collective-permute-done((bf16[128,1024]{1,0:T(8,128)(2,1)S(1)}, bf16[128,1024]{1,0:T(8,128)(2,1)S(1)}, u32[]{:S(2)}, u32[]{:S(2)}) %collective-permute-start.2) | collective-permute-done | bytes 262176 | tf_op jit(solution)/shard_map/ppermute | solution.py:90
  24.4 1.4 %given_first.1 = (bf16[528,768]{1,0:T(8,128)(2,1)S(1)}, bf16[512,1024]{1,0:T(8,128)(2,1)S(1)}, bf16[512,1024]{1,0:T(8,128)(2,1)S(1)}, bf16[1024,768]{1,0:T(8,128)(2,1)S(1)}) custom-call(s32[1]{0:T(128)} %bitcast.info_ref, f32[1,2048]{1,0:T(1,128)S(1)} %copy-done.6, bf16[128,1024]{1,0:T(8,128)(2,1)S(1)} %get-tuple-element.34.refs_0_, ...), custom_call_target="tpu_custom_call" | custom-call | flops 805306368 | bytes 4194304 | tf_op jit(solution)/shard_map/given_first/pallas_call | solution.py:226
  25.8 1.7 %collective-permute-start.5 = (bf16[528,768]{1,0:T(8,128)(2,1)S(1)}, bf16[528,768]{1,0:T(8,128)(2,1)S(1)}, u32[]{:S(2)}, u32[]{:S(2)}) collective-permute-start(bf16[528,768]{1,0:T(8,128)(2,1)S(1)} %get-tuple-element.42.refs_1_), channel_id=1, source_target_pairs={{0,2},{1,3},{2,0},{3,1},{4,5},{5,4},{6,7},{7,6},{8,10},{9,11},{10,... | collective-permute-start | bytes 2433032 | tf_op jit(solution)/shard_map/ppermute | solution.py:90
  28.1 9.8 %collective-permute-done.4.refs_1_ = bf16[512,768]{1,0:T(8,128)(2,1)S(1)} collective-permute-done((bf16[512,768]{1,0:T(8,128)(2,1)S(1)}, bf16[512,768]{1,0:T(8,128)(2,1)S(1)}, u32[]{:S(2)}, u32[]{:S(2)}) %collective-permute-start.4) | collective-permute-done | bytes 786464 | tf_op jit(solution)/shard_map/ppermute | solution.py:90
  39.0 1.7 %collective-permute-done.5.refs_2_ = bf16[528,768]{1,0:T(8,128)(2,1)S(1)} collective-permute-done((bf16[528,768]{1,0:T(8,128)(2,1)S(1)}, bf16[528,768]{1,0:T(8,128)(2,1)S(1)}, u32[]{:S(2)}, u32[]{:S(2)}) %collective-permute-start.5) | collective-permute-done | bytes 811040 | tf_op jit(solution)/shard_map/ppermute | solution.py:90
  40.7 1.6 %attend_first.1 = (bf16[256,256]{1,0:T(8,128)(2,1)S(1)}, bf16[256,256]{1,0:T(8,128)(2,1)S(1)}, f32[2,128,128]{2,1,0:T(8,128)S(1)}) custom-call(s32[1]{0:T(128)} %bitcast.info_ref, f32[512,768]{1,0:T(8,128)S(1)} %get-tuple-element.41.refs_0_, bf16[528,768]{1,0:T(8,128)(2,1)S(1)} %get-tuple-element.42.refs_1_, ...), custom_call_target="tpu_custom_call" | custom-call | flops 167772160 | bytes 8388608 | tf_op jit(solution)/shard_map/attend_first/pallas_call | solution.py:343
  42.3 1.8 %collective-permute-start.8 = (bf16[256,256]{1,0:T(8,128)(2,1)S(1)}, bf16[256,256]{1,0:T(8,128)(2,1)S(1)}, u32[]{:S(2)}, u32[]{:S(2)}) collective-permute-start(bf16[256,256]{1,0:T(8,128)(2,1)S(1)} %get-tuple-element.46.refs_0_), channel_id=1, source_target_pairs={{0,2},{1,3},{2,0},{3,1},{4,5},{5,4},{6,7},{7,6},{8,10},{9,11},{10,... | collective-permute-start | bytes 393224 | tf_op jit(solution)/shard_map/ppermute | solution.py:90
  44.8 1.5 %collective-permute-done.7.refs_3_.refs_5_ = bf16[256,1024]{1,0:T(8,128)(2,1)S(1)} collective-permute-done((bf16[256,1024]{1,0:T(8,128)(2,1)S(1)}, bf16[256,1024]{1,0:T(8,128)(2,1)S(1)}, u32[]{:S(2)}, u32[]{:S(2)}) %collective-permute-start.7) | collective-permute-done | bytes 524320 | tf_op jit(solution)/shard_map/ppermute | solution.py:90
  46.3 1.4 %collective-permute-done.8.refs_1_ = bf16[256,256]{1,0:T(8,128)(2,1)S(1)} collective-permute-done((bf16[256,256]{1,0:T(8,128)(2,1)S(1)}, bf16[256,256]{1,0:T(8,128)(2,1)S(1)}, u32[]{:S(2)}, u32[]{:S(2)}) %collective-permute-start.8) | collective-permute-done | bytes 131104 | tf_op jit(solution)/shard_map/ppermute | solution.py:90
  48.1 1.8 %collective-permute-start.13 = (bf16[256,512]{1,0:T(8,128)(2,1)S(1)}, bf16[256,512]{1,0:T(8,128)(2,1)S(1)}, u32[]{:S(2)}, u32[]{:S(2)}) collective-permute-start(bf16[256,512]{1,0:T(8,128)(2,1)S(1)} %get-tuple-element.51), channel_id=1, source_target_pairs={{0,1},{1,0},{2,3},{3,2},{4,6},{5,7},{6,4},{7,5},{8,9},{9,8},{10,11... | collective-permute-start | bytes 786440 | tf_op jit(solution)/shard_map/ppermute | solution.py:90
  49.9 1.5 %collective-permute-start.6 = (bf16[256,256]{1,0:T(8,128)(2,1)S(1)}, bf16[256,256]{1,0:T(8,128)(2,1)S(1)}, u32[]{:S(2)}, u32[]{:S(2)}) collective-permute-start(bf16[256,256]{1,0:T(8,128)(2,1)S(1)} %get-tuple-element.43.refs_0_), channel_id=1, source_target_pairs={{0,2},{1,3},{2,0},{3,1},{4,5},{5,4},{6,7},{7,6},{8,10},{9,11},{10,... | collective-permute-start | bytes 393224 | tf_op jit(solution)/shard_map/ppermute | solution.py:90
  52.0 4.3 %collective-permute-done.6.refs_1_ = bf16[256,256]{1,0:T(8,128)(2,1)S(1)} collective-permute-done((bf16[256,256]{1,0:T(8,128)(2,1)S(1)}, bf16[256,256]{1,0:T(8,128)(2,1)S(1)}, u32[]{:S(2)}, u32[]{:S(2)}) %collective-permute-start.6) | collective-permute-done | bytes 131104 | tf_op jit(solution)/shard_map/ppermute | solution.py:90
  59.7 2.3 %collective-permute-start.12 = (bf16[256,512]{1,0:T(8,128)(2,1)S(1)}, bf16[256,512]{1,0:T(8,128)(2,1)S(1)}, u32[]{:S(2)}, u32[]{:S(2)}) collective-permute-start(bf16[256,512]{1,0:T(8,128)(2,1)S(1)} %quarter_mine.1), channel_id=1, source_target_pairs={{0,6},{1,7},{2,4},{3,5},{4,9},{5,8},{6,11},{7,10},{8,14},{9,15},{1... | collective-permute-start | bytes 786440 | tf_op jit(solution)/shard_map/ppermute | solution.py:100
  62.0 3.5 %collective-permute-done.14.refs_2_ = bf16[256,512]{1,0:T(8,128)(2,1)S(1)} collective-permute-done((bf16[256,512]{1,0:T(8,128)(2,1)S(1)}, bf16[256,512]{1,0:T(8,128)(2,1)S(1)}, u32[]{:S(2)}, u32[]{:S(2)}) %collective-permute-start.14) | collective-permute-done | bytes 262176 | tf_op jit(solution)/shard_map/ppermute | solution.py:100
  66.4 1.8 %collective-permute-done.11.refs_0_ = bf16[256,512]{1,0:T(8,128)(2,1)S(1)} collective-permute-done((bf16[256,512]{1,0:T(8,128)(2,1)S(1)}, bf16[256,512]{1,0:T(8,128)(2,1)S(1)}, u32[]{:S(2)}, u32[]{:S(2)}) %collective-permute-start.11) | collective-permute-done | bytes 262176 | tf_op jit(solution)/shard_map/ppermute | solution.py:100
  68.3 3.3 %collective-permute-done.12.refs_1_ = bf16[256,512]{1,0:T(8,128)(2,1)S(1)} collective-permute-done((bf16[256,512]{1,0:T(8,128)(2,1)S(1)}, bf16[256,512]{1,0:T(8,128)(2,1)S(1)}, u32[]{:S(2)}, u32[]{:S(2)}) %collective-permute-start.12) | collective-permute-done | bytes 262176 | tf_op jit(solution)/shard_map/ppermute | solution.py:100
  71.6 2.7 %collective-permute-done.15.refs_3_ = bf16[256,512]{1,0:T(8,128)(2,1)S(1)} collective-permute-done((bf16[256,512]{1,0:T(8,128)(2,1)S(1)}, bf16[256,512]{1,0:T(8,128)(2,1)S(1)}, u32[]{:S(2)}, u32[]{:S(2)}) %collective-permute-start.15) | collective-permute-done | bytes 262176 | tf_op jit(solution)/shard_map/ppermute | solution.py:90
  74.3 1.4 %given_second.1 = (bf16[528,768]{1,0:T(8,128)(2,1)S(1)}, bf16[512,1024]{1,0:T(8,128)(2,1)S(1)}, bf16[512,1024]{1,0:T(8,128)(2,1)S(1)}) custom-call(s32[1]{0:T(128)} %bitcast.info_ref, f32[1,2048]{1,0:T(1,128)S(1)} %copy-done.6, bf16[256,512]{1,0:T(8,128)(2,1)S(1)} %collective-permute-done.11.refs_0_, bf16[256,512]{1,0:T(8,128)(2,1)S(1)} %collective-permute-done.12.refs_1_, ...), custom_call_target="tpu_custom_call" | custom-call | flops 805306368 | bytes 4194304 | tf_op jit(solution)/shard_map/given_second/pallas_call | solution.py:226
  77.3 10.7 %collective-permute-done.16.refs_2_ = bf16[528,768]{1,0:T(8,128)(2,1)S(1)} collective-permute-done((bf16[528,768]{1,0:T(8,128)(2,1)S(1)}, bf16[528,768]{1,0:T(8,128)(2,1)S(1)}, u32[]{:S(2)}, u32[]{:S(2)}) %collective-permute-start.16) | collective-permute-done | bytes 811040 | tf_op jit(solution)/shard_map/ppermute | solution.py:90
  88.0 1.6 %attend_second.1 = (bf16[256,256]{1,0:T(8,128)(2,1)S(1)}, bf16[384,256]{1,0:T(8,128)(2,1)S(1)}, f32[2,128,128]{2,1,0:T(8,128)S(1)}) custom-call(s32[1]{0:T(128)} %bitcast.info_ref, f32[512,768]{1,0:T(8,128)S(1)} %own_second.1.refs_0_, bf16[528,768]{1,0:T(8,128)(2,1)S(1)} %get-tuple-element.55.refs_1_, bf16[528,768]{1,0:T(8,128)(2,1)S(1)} %collective-permute-done.16.refs_2_, ...), custom_call_target="tpu_custom_call" | custom-call | flops 167772160 | bytes 8388608 | tf_op jit(solution)/shard_map/attend_second/pallas_call | solution.py:343
  90.2 1.5 %collective-permute-start.18 = (bf16[384,256]{1,0:T(8,128)(2,1)S(1)}, bf16[384,256]{1,0:T(8,128)(2,1)S(1)}, u32[]{:S(2)}, u32[]{:S(2)}) collective-permute-start(bf16[384,256]{1,0:T(8,128)(2,1)S(1)} %get-tuple-element.58.refs_2_), channel_id=1, source_target_pairs={{0,2},{1,3},{2,0},{3,1},{4,5},{5,4},{6,7},{7,6},{8,10},{9,11},{10,... | collective-permute-start | bytes 589832 | tf_op jit(solution)/shard_map/ppermute | solution.py:90
  91.7 4.3 %collective-permute-done.17.refs_1_ = bf16[256,256]{1,0:T(8,128)(2,1)S(1)} collective-permute-done((bf16[256,256]{1,0:T(8,128)(2,1)S(1)}, bf16[256,256]{1,0:T(8,128)(2,1)S(1)}, u32[]{:S(2)}, u32[]{:S(2)}) %collective-permute-start.17) | collective-permute-done | bytes 131104 | tf_op jit(solution)/shard_map/ppermute | solution.py:90
  97.5 2.7 %collective-permute-done.18.refs_3_.heads_ref = bf16[384,256]{1,0:T(8,128)(2,1)S(1)} collective-permute-done((bf16[384,256]{1,0:T(8,128)(2,1)S(1)}, bf16[384,256]{1,0:T(8,128)(2,1)S(1)}, u32[]{:S(2)}, u32[]{:S(2)}) %collective-permute-start.18) | collective-permute-done | bytes 196640 | tf_op jit(solution)/shard_map/ppermute | solution.py:90
  102.0 3.4 %collective-permute-done.20.got_ref = bf16[128,1024]{1,0:T(8,128)(2,1)S(1)} collective-permute-done((bf16[128,1024]{1,0:T(8,128)(2,1)S(1)}, bf16[128,1024]{1,0:T(8,128)(2,1)S(1)}, u32[]{:S(2)}, u32[]{:S(2)}) %collective-permute-start.20) | collective-permute-done | bytes 262176 | tf_op jit(solution)/shard_map/ppermute | solution.py:90
  105.5 4.3 %collective-permute-done.19.a_ref = bf16[192,1024]{1,0:T(8,128)(2,1)S(1)} collective-permute-done((bf16[192,1024]{1,0:T(8,128)(2,1)S(1)}, bf16[192,1024]{1,0:T(8,128)(2,1)S(1)}, u32[]{:S(2)}, u32[]{:S(2)}) %collective-permute-start.19) | collective-permute-done | bytes 393248 | tf_op jit(solution)/shard_map/ppermute | solution.py:90
  109.8 2.1 %collective-permute-done.21.b_ref = bf16[128,1024]{1,0:T(8,128)(2,1)S(1)} collective-permute-done((bf16[128,1024]{1,0:T(8,128)(2,1)S(1)}, bf16[128,1024]{1,0:T(8,128)(2,1)S(1)}, u32[]{:S(2)}, u32[]{:S(2)}) %collective-permute-start.21) | collective-permute-done | bytes 262176 | tf_op jit(solution)/shard_map/ppermute | solution.py:90
  (43 shorter events, 16.0 us)
Async XLA Ops:
  0.7 1.9 %copy-start.1 = (bf16[1,512,3072]{2,1,0:T(8,128)(2,1)S(1)}, bf16[1,512,3072]{2,1,0:T(8,128)(2,1)}, u32[]{:S(2)}) copy-start(bf16[1,512,3072]{2,1,0:T(8,128)(2,1)} %param.10) | copy-start | bytes 9437188
  2.5 3.4 %copy-start.3 = (bf16[1,128,2048]{2,1,0:T(8,128)(2,1)S(1)}, bf16[1,128,2048]{2,1,0:T(8,128)(2,1)}, u32[]{:S(2)}) copy-start(bf16[1,128,2048]{2,1,0:T(8,128)(2,1)} %param.7) | copy-start | bytes 1572868
  2.5 21.8 %copy-start.6 = (f32[1,2048]{1,0:T(1,128)S(1)}, f32[1,2048]{1,0:T(1,128)}, u32[]{:S(2)}) copy-start(f32[1,2048]{1,0:T(1,128)} %gain_ref.3) | copy-start | bytes 24580
  3.0 21.4 %collective-permute-start.3 = (bf16[512,768]{1,0:T(8,128)(2,1)S(1)}, bf16[512,768]{1,0:T(8,128)(2,1)S(1)}, u32[]{:S(2)}, u32[]{:S(2)}) collective-permute-start(bf16[512,768]{1,0:T(8,128)(2,1)S(1)} %get-tuple-element.37), channel_id=1, source_target_pairs={{0,1},{1,0},{2,3},{3,2},{4,6},{5,7},{6,4},{7,5},{8,9},{9,8},{10,11... | collective-permute-start | bytes 2359304 | tf_op jit(solution)/shard_map/ppermute | solution.py:90
  6.0 21.4 %copy-start.2 = (bf16[1,256,2048]{2,1,0:T(8,128)(2,1)S(1)}, bf16[1,256,2048]{2,1,0:T(8,128)(2,1)}, u32[]{:S(2)}) copy-start(bf16[1,256,2048]{2,1,0:T(8,128)(2,1)} %param.11) | copy-start | bytes 3145732
  6.0 21.4 %copy-start.4 = (bf16[128,2048]{1,0:T(8,128)(2,1)S(1)}, bf16[128,2048]{1,0:T(8,128)(2,1)}, u32[]{:S(2)}) copy-start(bf16[128,2048]{1,0:T(8,128)(2,1)} %refs_1_.1) | copy-start | bytes 1572868
  6.1 9.2 %collective-permute-start.1 = (bf16[128,1024]{1,0:T(8,128)(2,1)S(1)}, bf16[128,1024]{1,0:T(8,128)(2,1)S(1)}, u32[]{:S(2)}, u32[]{:S(2)}) collective-permute-start(bf16[128,1024]{1,0:T(8,128)(2,1)S(1)} %get-tuple-element.35), channel_id=1, source_target_pairs={{0,2},{1,3},{2,0},{3,1},{4,5},{5,4},{6,7},{7,6},{8,10},{9,11},{10,... | collective-permute-start | bytes 786440 | tf_op jit(solution)/shard_map/ppermute | solution.py:90
  7.6 13.9 %collective-permute-start = (bf16[128,1024]{1,0:T(8,128)(2,1)S(1)}, bf16[128,1024]{1,0:T(8,128)(2,1)S(1)}, u32[]{:S(2)}, u32[]{:S(2)}) collective-permute-start(bf16[128,1024]{1,0:T(8,128)(2,1)S(1)} %get-tuple-element.34.refs_0_), channel_id=1, source_target_pairs={{0,1},{1,0},{2,3},{3,2},{4,6},{5,7},{6,4},{7,5},{8,9},{9,8},{10,11... | collective-permute-start | bytes 786440 | tf_op jit(solution)/shard_map/ppermute | solution.py:90
  15.3 9.1 %collective-permute-start.2 = (bf16[128,1024]{1,0:T(8,128)(2,1)S(1)}, bf16[128,1024]{1,0:T(8,128)(2,1)S(1)}, u32[]{:S(2)}, u32[]{:S(2)}) collective-permute-start(bf16[128,1024]{1,0:T(8,128)(2,1)S(1)} %collective-permute-done.1.refs_2_), channel_id=1, source_target_pairs={{0,1},{1,0},{2,3},{3,2},{4,6},{5,7},{6,4},{7,5},{8,9},{9,8},{10,11... | collective-permute-start | bytes 786440 | tf_op jit(solution)/shard_map/ppermute | solution.py:90
  15.9 22.0 %collective-permute-start.4 = (bf16[512,768]{1,0:T(8,128)(2,1)S(1)}, bf16[512,768]{1,0:T(8,128)(2,1)S(1)}, u32[]{:S(2)}, u32[]{:S(2)}) collective-permute-start(bf16[512,768]{1,0:T(8,128)(2,1)S(1)} %get-tuple-element.40), channel_id=1, source_target_pairs={{0,1},{1,0},{2,3},{3,2},{4,6},{5,7},{6,4},{7,5},{8,9},{9,8},{10,11... | collective-permute-start | bytes 2359304 | tf_op jit(solution)/shard_map/ppermute | solution.py:90
  25.8 14.9 %collective-permute-start.5 = (bf16[528,768]{1,0:T(8,128)(2,1)S(1)}, bf16[528,768]{1,0:T(8,128)(2,1)S(1)}, u32[]{:S(2)}, u32[]{:S(2)}) collective-permute-start(bf16[528,768]{1,0:T(8,128)(2,1)S(1)} %get-tuple-element.42.refs_1_), channel_id=1, source_target_pairs={{0,2},{1,3},{2,0},{3,1},{4,5},{5,4},{6,7},{7,6},{8,10},{9,11},{10,... | collective-permute-start | bytes 2433032 | tf_op jit(solution)/shard_map/ppermute | solution.py:90
  27.6 13.1 %copy-start = (f32[1,8,128,128]{3,2,1,0:T(8,128)S(1)}, f32[1,8,128,128]{3,2,1,0:T(8,128)}, u32[]{:S(2)}) copy-start(f32[1,8,128,128]{3,2,1,0:T(8,128)} %param.9) | copy-start | bytes 1572868
  27.6 13.1 %copy-start.5 = (f32[1,1024]{1,0:T(1,128)S(1)}, f32[1,1024]{1,0:T(1,128)}, u32[]{:S(2)}) copy-start(f32[1,1024]{1,0:T(1,128)} %refs_4_.3) | copy-start | bytes 12292
  27.6 18.7 %collective-permute-start.7 = (bf16[256,1024]{1,0:T(8,128)(2,1)S(1)}, bf16[256,1024]{1,0:T(8,128)(2,1)S(1)}, u32[]{:S(2)}, u32[]{:S(2)}) collective-permute-start(bf16[256,1024]{1,0:T(8,128)(2,1)S(1)} %get-tuple-element.45), channel_id=1, source_target_pairs={{0,2},{1,3},{2,0},{3,1},{4,5},{5,4},{6,7},{7,6},{8,10},{9,11},{10,... | collective-permute-start | bytes 1572872 | tf_op jit(solution)/shard_map/ppermute | solution.py:90
  42.3 5.4 %collective-permute-start.8 = (bf16[256,256]{1,0:T(8,128)(2,1)S(1)}, bf16[256,256]{1,0:T(8,128)(2,1)S(1)}, u32[]{:S(2)}, u32[]{:S(2)}) collective-permute-start(bf16[256,256]{1,0:T(8,128)(2,1)S(1)} %get-tuple-element.46.refs_0_), channel_id=1, source_target_pairs={{0,2},{1,3},{2,0},{3,1},{4,5},{5,4},{6,7},{7,6},{8,10},{9,11},{10,... | collective-permute-start | bytes 393224 | tf_op jit(solution)/shard_map/ppermute | solution.py:90
  44.1 12.6 %collective-permute-start.10 = (bf16[128,1024]{1,0:T(8,128)(2,1)S(1)}, bf16[128,1024]{1,0:T(8,128)(2,1)S(1)}, u32[]{:S(2)}, u32[]{:S(2)}) collective-permute-start(bf16[128,1024]{1,0:T(8,128)(2,1)S(1)} %get-tuple-element.50), channel_id=1, source_target_pairs={{28,29},{29,28},{30,31},{31,30}} | collective-permute-start | bytes 786440 | tf_op jit(solution)/shard_map/ppermute | solution.py:90
  48.1 8.6 %collective-permute-start.13 = (bf16[256,512]{1,0:T(8,128)(2,1)S(1)}, bf16[256,512]{1,0:T(8,128)(2,1)S(1)}, u32[]{:S(2)}, u32[]{:S(2)}) collective-permute-start(bf16[256,512]{1,0:T(8,128)(2,1)S(1)} %get-tuple-element.51), channel_id=1, source_target_pairs={{0,1},{1,0},{2,3},{3,2},{4,6},{5,7},{6,4},{7,5},{8,9},{9,8},{10,11... | collective-permute-start | bytes 786440 | tf_op jit(solution)/shard_map/ppermute | solution.py:90
  49.9 6.4 %collective-permute-start.6 = (bf16[256,256]{1,0:T(8,128)(2,1)S(1)}, bf16[256,256]{1,0:T(8,128)(2,1)S(1)}, u32[]{:S(2)}, u32[]{:S(2)}) collective-permute-start(bf16[256,256]{1,0:T(8,128)(2,1)S(1)} %get-tuple-element.43.refs_0_), channel_id=1, source_target_pairs={{0,2},{1,3},{2,0},{3,1},{4,5},{5,4},{6,7},{7,6},{8,10},{9,11},{10,... | collective-permute-start | bytes 393224 | tf_op jit(solution)/shard_map/ppermute | solution.py:90
  51.4 7.4 %collective-permute-start.9 = (bf16[256,512]{1,0:T(8,128)(2,1)S(1)}, bf16[256,512]{1,0:T(8,128)(2,1)S(1)}, u32[]{:S(2)}, u32[]{:S(2)}) collective-permute-start(bf16[256,512]{1,0:T(8,128)(2,1)S(1)} %get-tuple-element.47), channel_id=1, source_target_pairs={{0,1},{1,0},{2,3},{3,2},{4,6},{5,7},{6,4},{7,5},{8,9},{9,8},{10,11... | collective-permute-start | bytes 786440 | tf_op jit(solution)/shard_map/ppermute | solution.py:90
  56.9 8.6 %collective-permute-start.14 = (bf16[256,512]{1,0:T(8,128)(2,1)S(1)}, bf16[256,512]{1,0:T(8,128)(2,1)S(1)}, u32[]{:S(2)}, u32[]{:S(2)}) collective-permute-start(bf16[256,512]{1,0:T(8,128)(2,1)S(1)} %quarter_other.1), channel_id=1, source_target_pairs={{0,5},{1,4},{2,7},{3,6},{4,10},{5,11},{6,8},{7,9},{8,13},{9,12},{1... | collective-permute-start | bytes 786440 | tf_op jit(solution)/shard_map/ppermute | solution.py:100
  58.9 9.4 %collective-permute-start.11 = (bf16[256,512]{1,0:T(8,128)(2,1)S(1)}, bf16[256,512]{1,0:T(8,128)(2,1)S(1)}, u32[]{:S(2)}, u32[]{:S(2)}) collective-permute-start(bf16[256,512]{1,0:T(8,128)(2,1)S(1)} %quarter_mine.1), channel_id=1, source_target_pairs={{0,4},{1,5},{2,6},{3,7},{4,8},{5,9},{6,10},{7,11},{8,12},{9,13},{1... | collective-permute-start | bytes 786440 | tf_op jit(solution)/shard_map/ppermute | solution.py:100
  59.7 11.8 %collective-permute-start.12 = (bf16[256,512]{1,0:T(8,128)(2,1)S(1)}, bf16[256,512]{1,0:T(8,128)(2,1)S(1)}, u32[]{:S(2)}, u32[]{:S(2)}) collective-permute-start(bf16[256,512]{1,0:T(8,128)(2,1)S(1)} %quarter_mine.1), channel_id=1, source_target_pairs={{0,6},{1,7},{2,4},{3,5},{4,9},{5,8},{6,11},{7,10},{8,14},{9,15},{1... | collective-permute-start | bytes 786440 | tf_op jit(solution)/shard_map/ppermute | solution.py:100
  65.5 8.8 %collective-permute-start.15 = (bf16[256,512]{1,0:T(8,128)(2,1)S(1)}, bf16[256,512]{1,0:T(8,128)(2,1)S(1)}, u32[]{:S(2)}, u32[]{:S(2)}) collective-permute-start(bf16[256,512]{1,0:T(8,128)(2,1)S(1)} %collective-permute-done.14.refs_2_), channel_id=1, source_target_pairs={{0,1},{1,0},{2,3},{3,2},{4,6},{5,7},{6,4},{7,5},{8,9},{9,8},{10,11... | collective-permute-start | bytes 786440 | tf_op jit(solution)/shard_map/ppermute | solution.py:90
  75.6 12.3 %collective-permute-start.16 = (bf16[528,768]{1,0:T(8,128)(2,1)S(1)}, bf16[528,768]{1,0:T(8,128)(2,1)S(1)}, u32[]{:S(2)}, u32[]{:S(2)}) collective-permute-start(bf16[528,768]{1,0:T(8,128)(2,1)S(1)} %get-tuple-element.55.refs_1_), channel_id=1, source_target_pairs={{0,2},{1,3},{2,0},{3,1},{4,5},{5,4},{6,7},{7,6},{8,10},{9,11},{10,... | collective-permute-start | bytes 2433032 | tf_op jit(solution)/shard_map/ppermute | solution.py:90
  89.6 6.4 %collective-permute-start.17 = (bf16[256,256]{1,0:T(8,128)(2,1)S(1)}, bf16[256,256]{1,0:T(8,128)(2,1)S(1)}, u32[]{:S(2)}, u32[]{:S(2)}) collective-permute-start(bf16[256,256]{1,0:T(8,128)(2,1)S(1)} %get-tuple-element.57.refs_0_), channel_id=1, source_target_pairs={{0,2},{1,3},{2,0},{3,1},{4,5},{5,4},{6,7},{7,6},{8,10},{9,11},{10,... | collective-permute-start | bytes 393224 | tf_op jit(solution)/shard_map/ppermute | solution.py:90
  90.2 10.0 %collective-permute-start.18 = (bf16[384,256]{1,0:T(8,128)(2,1)S(1)}, bf16[384,256]{1,0:T(8,128)(2,1)S(1)}, u32[]{:S(2)}, u32[]{:S(2)}) collective-permute-start(bf16[384,256]{1,0:T(8,128)(2,1)S(1)} %get-tuple-element.58.refs_2_), channel_id=1, source_target_pairs={{0,2},{1,3},{2,0},{3,1},{4,5},{5,4},{6,7},{7,6},{8,10},{9,11},{10,... | collective-permute-start | bytes 589832 | tf_op jit(solution)/shard_map/ppermute | solution.py:90
  96.3 9.0 %collective-permute-start.20 = (bf16[128,1024]{1,0:T(8,128)(2,1)S(1)}, bf16[128,1024]{1,0:T(8,128)(2,1)S(1)}, u32[]{:S(2)}, u32[]{:S(2)}) collective-permute-start(bf16[128,1024]{1,0:T(8,128)(2,1)S(1)} %crossing.1), channel_id=1, source_target_pairs={{0,1},{1,0},{2,3},{3,2},{4,6},{5,7},{6,4},{7,5},{8,9},{9,8},{10,11... | collective-permute-start | bytes 786440 | tf_op jit(solution)/shard_map/ppermute | solution.py:90
  100.8 9.0 %collective-permute-start.19 = (bf16[192,1024]{1,0:T(8,128)(2,1)S(1)}, bf16[192,1024]{1,0:T(8,128)(2,1)S(1)}, u32[]{:S(2)}, u32[]{:S(2)}) collective-permute-start(bf16[192,1024]{1,0:T(8,128)(2,1)S(1)} %get-tuple-element.61), channel_id=1, source_target_pairs={{0,1},{1,0},{2,3},{3,2},{4,6},{5,7},{6,4},{7,5},{8,9},{9,8},{10,11... | collective-permute-start | bytes 1179656 | tf_op jit(solution)/shard_map/ppermute | solution.py:90
  105.4 6.4 %collective-permute-start.21 = (bf16[128,1024]{1,0:T(8,128)(2,1)S(1)}, bf16[128,1024]{1,0:T(8,128)(2,1)S(1)}, u32[]{:S(2)}, u32[]{:S(2)}) collective-permute-start(bf16[128,1024]{1,0:T(8,128)(2,1)S(1)} %combine.1), channel_id=1, source_target_pairs={{0,2},{1,3},{2,0},{3,1},{4,5},{5,4},{6,7},{7,6},{8,10},{9,11},{10,... | collective-permute-start | bytes 786440 | tf_op jit(solution)/shard_map/ppermute | solution.py:90
